TPU v7x, 256 devices: a whole 4x4x8 slice. The times are simulated.
256 devices in a mesh: seq: 32 (over z, y), head: 8 (over x, core).
Axes of the slice: x: 4, y: 4, z: 8, core: 2. Of those that a mesh axis runs over, the one named last changes fastest.
Arguments:
- queries: bfloat16 [32768, 12288], P(('seq', 'head')), may hold values from -8 to 8
- latent: bfloat16 [32768, 512], P(('seq', 'head')), may hold values from -6 to 6
- rope_keys: bfloat16 [32768, 64], P(('seq', 'head')), may hold values from -8 to 8
- key_weight: bfloat16 [512, 8192], P('seq', 'head'), may hold values from -0.25 to 0.25
- value_weight: bfloat16 [512, 8192], P('seq', 'head'), may hold values from -0.25 to 0.25
- doc_lengths: int32 [128], replicated, may hold values from 1 to 510, as said below
Outputs:
- attended: bfloat16 [32768, 8192], P(('seq', 'head'))
Inputs may be any that keep to these rules, and one draw needn't show every extreme that they name: `doc_lengths`: the documents lie in order in the pack and their lengths sum to 32768; document 0 starts at position 0 and every other document d starts strictly inside positions d * 256 to (d + 1) * 256 - 1, excluding the first of these; one length is exactly 510.
All inputs are finite; a program needn't handle non-finite values.
Results may differ from a plain program's by a relative error of at most 0.0062.
Values may be sent and summed in bfloat16 or wider, within the bound.
A program may use at most 64 MiB of HBM per device.

v0:
```python
import math

import jax
import jax.numpy as jnp
from jax import lax
from jax.sharding import Mesh
from jax.sharding import PartitionSpec as P

NOPE = 128
ROPE = 64
VDIM = 128
SEQ = ("seq_0", "seq_1")
SEQ_HEAD = ("seq_0", "seq_1", "head")


lowest_score = -1e30


def sent_together(arrays, axis, dim, along):
    both = jnp.concatenate(arrays, axis=along)
    out, at, finished = (lax.all_gather(both, axis, axis=dim, tiled=True), 0, [])
    for a in arrays:
        finished.append(lax.slice_in_dim(out, at, at + a.shape[along], axis=along))
        at += a.shape[along]
    return tuple(finished)


def shifted(value, axis, steps):
    count = lax.axis_size(axis)
    first, last = (max(0, -steps), min(count, count - steps))
    return lax.ppermute(value, axis, [(source, source + steps) for source in range(first, last)])


def gathered_by_axis(shard, axes, dim):
    if not axes:
        return shard
    nearer = lax.all_gather(shard, axes[-1], axis=dim, tiled=True)
    return gathered_by_axis(nearer, axes[:-1], dim)


def document_of(doc_lengths, first_place, count):
    starts = jnp.cumsum(doc_lengths) - doc_lengths
    places = first_place + jnp.arange(count, dtype=jnp.int32)
    started = (starts[None, :] <= places[:, None]).astype(jnp.int32)
    return jnp.sum(started, axis=1) - 1


def shards(queries, latent, rope_keys, key_weight, value_weight, doc_lengths):
    tok_rows = queries.shape[0]
    groups = lax.axis_size("head")
    group_rows = tok_rows * groups
    local_heads = key_weight.shape[1] // NOPE
    qk_width = NOPE + ROPE
    block_rows = min(512, group_rows)
    score_scale = 1.0 / math.sqrt(qk_width)
    group_latent, group_rope = sent_together((latent, rope_keys), "head", 0, 1)
    by_heads = queries.reshape(tok_rows, groups, local_heads * qk_width)
    my_queries = lax.all_to_all(by_heads, "head", split_axis=1, concat_axis=0, tiled=True)
    my_queries = my_queries.reshape(group_rows, local_heads, qk_width)
    earlier_latent, earlier_rope = shifted((group_latent, group_rope), SEQ, 1)
    latent_rows = jnp.concatenate([earlier_latent, group_latent], axis=0)
    key_sums = jnp.dot(
        latent_rows, gathered_by_axis(key_weight, SEQ, 0), preferred_element_type=jnp.float32
    )
    value_sums = jnp.dot(
        latent_rows, gathered_by_axis(value_weight, SEQ, 0), preferred_element_type=jnp.float32
    )
    keys_all = key_sums.astype(jnp.bfloat16)
    values_all = value_sums.astype(jnp.bfloat16)
    rope_all = jnp.concatenate([earlier_rope, group_rope], axis=0)
    first_place = lax.axis_index(SEQ) * group_rows - group_rows
    key_docs = document_of(doc_lengths, first_place, 2 * group_rows)
    key_blocks = group_rows // block_rows + 1

    def one_block(q_index):
        q_start = q_index * block_rows
        q_block = lax.dynamic_slice_in_dim(my_queries, q_start, block_rows, 0)
        q_nope = q_block[:, :, :NOPE]
        q_rope = q_block[:, :, NOPE:]
        q_docs = lax.dynamic_slice_in_dim(key_docs, group_rows + q_start, block_rows, 0)
        q_places = group_rows + q_start + jnp.arange(block_rows, dtype=jnp.int32)

        def attend(state_now, k_start):
            row_peak, row_sum, weighted = state_now
            k_nope = lax.dynamic_slice_in_dim(keys_all, k_start, block_rows, 0).reshape(
                block_rows, local_heads, NOPE
            )
            k_rope = lax.dynamic_slice_in_dim(rope_all, k_start, block_rows, 0)
            k_values = lax.dynamic_slice_in_dim(values_all, k_start, block_rows, 0).reshape(
                block_rows, local_heads, VDIM
            )
            k_docs = lax.dynamic_slice_in_dim(key_docs, k_start, block_rows, 0)
            k_places = k_start + jnp.arange(block_rows, dtype=jnp.int32)
            scores = jnp.einsum("ihd,jhd->hij", q_nope, k_nope, preferred_element_type=jnp.float32)
            scores = (
                scores
                + jnp.einsum("ihd,jd->hij", q_rope, k_rope, preferred_element_type=jnp.float32)
            ) * score_scale
            allowed = (q_docs[:, None] == k_docs[None, :]) & (
                k_places[None, :] <= q_places[:, None]
            )
            scores = jnp.where(allowed[None, :, :], scores, -jnp.inf)
            new_peak = jnp.maximum(row_peak, jnp.max(scores, axis=2))
            expo = jnp.exp(scores - new_peak[:, :, None])
            rescale = jnp.exp(row_peak - new_peak)
            row_sum = row_sum * rescale + jnp.sum(expo, axis=2)
            rounded = expo.astype(jnp.bfloat16)
            weighted = weighted * jnp.transpose(rescale)[:, :, None] + jnp.einsum(
                "hij,jhd->ihd", rounded, k_values, preferred_element_type=jnp.float32
            )
            return (new_peak, row_sum, weighted)

        def skip_block(state_now, k_start):
            return state_now

        def visit(k_index, state_now):
            k_start = (q_index + k_index) * block_rows
            needed = key_docs[k_start + block_rows - 1] >= q_docs[0]
            return lax.cond(needed, attend, skip_block, state_now, k_start)

        start_state = (
            jnp.full((local_heads, block_rows), lowest_score, jnp.float32),
            jnp.zeros((local_heads, block_rows), jnp.float32),
            jnp.zeros((block_rows, local_heads, VDIM), jnp.float32),
        )
        row_peak, row_sum, weighted = lax.fori_loop(0, key_blocks, visit, start_state)
        mixed = weighted / jnp.transpose(row_sum)[:, :, None]
        return mixed.reshape(block_rows, local_heads * VDIM).astype(jnp.bfloat16)

    attended = lax.map(one_block, jnp.arange(group_rows // block_rows, dtype=jnp.int32))
    attended = attended.reshape(group_rows, local_heads * VDIM)
    return lax.all_to_all(attended, "head", split_axis=0, concat_axis=1, tiled=True)


def solution(mesh):
    torus = Mesh(mesh.devices.reshape(8, 4, mesh.shape["head"]), ("seq_0", "seq_1", "head"))
    in_specs = (
        P(SEQ_HEAD, None),
        P(SEQ_HEAD, None),
        P(SEQ_HEAD, None),
        P(SEQ, "head"),
        P(SEQ, "head"),
        P(),
    )
    out_specs = P(SEQ_HEAD, None)
    return jax.shard_map(
        shards, mesh=torus, in_specs=in_specs, out_specs=out_specs, check_vma=False
    )
```

profile of v0, /device:TPU:8, one launch (start us, length us, event | category | flops | bytes accessed | tf_op | source)
XLA Modules:
  0.0 255.5 jit_solution(15252564446096518743)
XLA Ops:
  6.5 1.0 copy.62
  7.6 1.4 pad_maximum_fusion.4
  9.0 13.2 %all_gather.16 = bf16[64,1024]{1,0:T(8,128)(2,1)} all-gather(bf16[16,1024]{1,0:T(8,128)(2,1)} %param.15), channel_id=1, replica_groups=mesh['seq_0'=8,'seq_1'=4,'head'=8] {'seq_1'}, dimensions={0}, use_global_device_ids=true | all-gather | bytes 163840 | tf_op jit(solution)/shard_map/all_gather | solution.py:37
  22.3 4.7 %copy.60 = bf16[128,12288]{0,1:T(8,128)(2,1)} copy(bf16[128,12288]{1,0:T(8,128)(2,1)} %param.12) | data formatting | bytes 6291456 | tf_op args[0]
  27.0 4.4 %all-to-all-start = ((bf16[128,8,1536]{0,2,1:T(8,128)(2,1)}), bf16[128,8,1536]{0,2,1:T(8,128)(2,1)S(1)}, u32[]{:S(2)}, u32[]{:S(2)}) async-start(bf16[128,8,1536]{0,2,1:T(8,128)(2,1)} %bitcast.52), calls=%async_computation | async-start | bytes 6291456 | tf_op jit(solution)/shard_map/all_to_all | solution.py:58
  31.4 12.7 %all_gather.18 = bf16[64,1024]{1,0:T(8,128)(2,1)} all-gather(bf16[16,1024]{1,0:T(8,128)(2,1)S(1)} %copy-done.1), channel_id=1, replica_groups=mesh['seq_0'=8,'seq_1'=4,'head'=8] {'seq_1'}, dimensions={0}, use_global_device_ids=true | all-gather | bytes 163840 | tf_op jit(solution)/shard_map/all_gather | solution.py:37
  44.2 2.4 slice.39
  46.5 2.7 %collective-permute-start = (bf16[1024,512]{0,1:T(8,128)(2,1)}, bf16[1024,512]{0,1:T(8,128)(2,1)}, u32[]{:S(2)}, u32[]{:S(2)}) collective-permute-start(bf16[1024,512]{0,1:T(8,128)(2,1)} %slice.39), channel_id=1, source_target_pairs={{0,8},{8,16},{16,24},{24,32},{32,40},{40,48},{48,56},{56,64},{64,7... | collective-permute-start | bytes 3145736 | tf_op jit(solution)/shard_map/ppermute | solution.py:31
  50.3 0.9 slice.40
  51.2 3.8 %collective-permute-start.1 = (bf16[1024,64]{0,1:T(8,128)(2,1)S(1)}, bf16[1024,64]{0,1:T(8,128)(2,1)S(1)}, u32[]{:S(2)}, u32[]{:S(2)}) collective-permute-start(bf16[1024,64]{0,1:T(8,128)(2,1)S(1)} %slice.40), channel_id=1, source_target_pairs={{0,8},{8,16},{16,24},{24,32},{32,40},{40,48},{48,56},{56,64},{64,7... | collective-permute-start | bytes 393224 | tf_op jit(solution)/shard_map/ppermute | solution.py:31
  55.0 19.7 %collective-permute-done.1 = bf16[1024,64]{0,1:T(8,128)(2,1)S(1)} collective-permute-done((bf16[1024,64]{0,1:T(8,128)(2,1)S(1)}, bf16[1024,64]{0,1:T(8,128)(2,1)S(1)}, u32[]{:S(2)}, u32[]{:S(2)}) %collective-permute-start.1) | collective-permute-done | bytes 131104 | tf_op jit(solution)/shard_map/ppermute | solution.py:31
  74.8 10.2 %copy.61 = bf16[8,128,1,1536]{1,0,3,2:T(8,128)(2,1)} copy(bf16[8,128,1,1536]{1,3,0,2:T(8,128)(2,1)S(1)} %bitcast.51) | data formatting | bytes 6291456 | tf_op jit(solution)/shard_map/all_to_all | solution.py:58
  85.0 5.8 %reshape.134 = bf16[1024,8,192]{0,2,1:T(8,128)(2,1)} reshape(bf16[8,128,1,1536]{1,0,3,2:T(8,128)(2,1)} %copy.61) | data formatting | bytes 6291456 | tf_op jit(solution)/shard_map/reshape | solution.py:59
  90.8 6.3 %convolution_convert_fusion.1 = bf16[2048,1024]{1,0:T(8,128)(2,1)} fusion(bf16[512,1024]{1,0:T(8,128)(2,1)} %all-gather.6.cloned.1.call-done, bf16[1024,512]{0,1:T(8,128)(2,1)} %slice.39, bf16[1024,512]{0,1:T(8,128)(2,1)} %collective-permute-done), kind=kOutput, calls=%fused_computation.27 | convolution fusion | flops 2153775104 | bytes 7340032 | tf_op jit(solution)/shard_map/dot_general | solution.py:62
  97.1 6.5 %copy.63 = bf16[2048,1024]{0,1:T(8,128)(2,1)} copy(bf16[2048,1024]{1,0:T(8,128)(2,1)} %convolution_convert_fusion.1) | data formatting | bytes 8388608 | tf_op jit(solution)/shard_map/while | solution.py:130
  103.6 19.0 %all-gather.8.cloned.1.call-done = bf16[512,1024]{1,0:T(8,128)(2,1)} async-done(((bf16[64,1024]{1,0:T(8,128)(2,1)}), bf16[512,1024]{1,0:T(8,128)(2,1)}) %all-gather.8.cloned.1.call-update) | async-done | bytes 1048592 | tf_op jit(solution)/shard_map/all_gather | solution.py:37
  122.6 6.3 %convolution_convert_fusion = bf16[2048,1024]{1,0:T(8,128)(2,1)} fusion(bf16[512,1024]{1,0:T(8,128)(2,1)} %all-gather.8.cloned.1.call-done, bf16[1024,512]{0,1:T(8,128)(2,1)} %slice.39, bf16[1024,512]{0,1:T(8,128)(2,1)} %collective-permute-done), kind=kOutput, calls=%fused_computation.26 | convolution fusion | flops 2153775104 | bytes 7340032 | tf_op jit(solution)/shard_map/dot_general | solution.py:65
  128.9 6.5 %copy.64 = bf16[2048,1024]{0,1:T(8,128)(2,1)} copy(bf16[2048,1024]{1,0:T(8,128)(2,1)} %convolution_convert_fusion) | data formatting | bytes 8388608 | tf_op jit(solution)/shard_map/while | solution.py:130
  135.4 75.7 %while.55 = (s32[]{:T(128)}, bf16[2,512,1024]{2,1,0:T(8,128)(2,1)}, s32[2]{0:T(128)S(1)}, s32[2048]{0:T(1024)S(1)}, bf16[1024,8,192]{0,2,1:T(8,128)(2,1)}, /*ind...) while((s32[]{:T(128)}, bf16[2,512,1024]{2,1,0:T(8,128)(2,1)}, ...), condition=%wide.region_9.10_spmd, body=%wide.region_2.9_spmd.sunk | while | flops 1361851392 | bytes 71706064 | solution.py:130
  135.4 0.6 dynamic_slice.62
  136.6 1.9 constant_dynamic-slice_fusion.7
  138.6 1.3 constant_dynamic-slice_fusion.6
  140.0 0.7 copy.74
  140.9 30.5 %while.56 = (s32[]{:T(128)}, f32[8,512]{1,0:T(8,128)S(1)}, f32[8,512]{1,0:T(8,128)S(1)}, f32[512,8,128]{0,2,1:T(8,128)S(1)}, s32[]{:T(128)}, /*index=5*/s32[2048...) while((s32[]{:T(128)}, f32[8,512]{1,0:T(8,128)S(1)}, ...), condition=%wide.region_8.8_spmd.clone, body=%wide.region_3.7_spmd.clone.sunk | while | flops 1360802816 | bytes 56971772 | solution.py:126
  141.6 0.7 dynamic_slice.64
  144.8 0.7 dynamic_slice.64
  147.3 10.4 %conditional.3 = ((f32[8,512]{1,0:T(8,128)S(1)}, f32[8,512]{1,0:T(8,128)S(1)}, f32[512,8,128]{0,2,1:T(8,128)S(1)})) conditional(s32[]{:T(128)} %bitcast.46, (f32[8,512]{1,0:T(8,128)S(1)}, f32[8,512]{1,0:T(8,128)S(1)}, f32[512,8,128]{0,2,1:T(8,128)S(1)}) %tuple.116, (s32[512]{0:T(512)S(1)}, s32[]{:T(128)}, s32[2048]{0:T(1024)S(1)}, s32[]{:T(128)}, ...), branch_computations={%region_4.3_spmd, %region_5.6_spmd} | conditional | flops 1360802816 | bytes 56969328 | solution.py:119
  147.7 2.8 %constant_dynamic-slice_fusion = (bf16[512,1024]{0,1:T(8,128)(2,1)S(1)}, bf16[512,1024]{0,1:T(8,128)(2,1)S(1)}) fusion(bf16[2048,1024]{0,1:T(8,128)(2,1)} %get-tuple-element.657, s32[]{:T(128)S(6)} %select_n.35, bf16[2048,1024]{0,1:T(8,128)(2,1)} %get-tuple-element.651), kind=kLoop, calls=%fused_computation.19 | loop fusion | bytes 4194308 | tf_op jit(solution)/shard_map/while/body/eval_jaxpr/while/body/eval_jaxpr/cond/branch_1_fun/dynamic_slice | solution.py:89
  150.5 1.4 fusion.11
  151.9 2.7 %fusion.18 = (f32[8,512]{1,0:T(8,128)S(1)}, f32[8,512,512]{1,2,0:T(8,128)S(1)}) fusion(f32[512,512,8]{1,0,2:T(8,128)S(1)} %fusion.11, bf16[512,8,128]{0,2,1:T(8,128)(2,1)S(1)} %bitcast.48, bf16[512,8,128]{2,0,1:T(8,128)(2,1)S(1)} %get-tuple-element.652, pred[512,512]{0,1:T(8,128)(4,1)S(1)} %compare_and_fusion), kind=kOutput, calls=%fused_computation.36 | convolution fusion | flops 545255424 | bytes 19152896 | tf_op jit(solution)/shard_map/while/body/eval_jaxpr/while/body/eval_jaxpr/cond/branch_1_fun/ihd,jhd->hij/dot_general | solution.py:94
  154.6 2.0 bitcast_add_fusion.1
  156.6 1.2 fusion.5
  158.4 0.7 dynamic_slice.64
  160.9 10.4 %conditional.3 = ((f32[8,512]{1,0:T(8,128)S(1)}, f32[8,512]{1,0:T(8,128)S(1)}, f32[512,8,128]{0,2,1:T(8,128)S(1)})) conditional(s32[]{:T(128)} %bitcast.46, (f32[8,512]{1,0:T(8,128)S(1)}, f32[8,512]{1,0:T(8,128)S(1)}, f32[512,8,128]{0,2,1:T(8,128)S(1)}) %tuple.116, (s32[512]{0:T(512)S(1)}, s32[]{:T(128)}, s32[2048]{0:T(1024)S(1)}, s32[]{:T(128)}, ...), branch_computations={%region_4.3_spmd, %region_5.6_spmd} | conditional | flops 1360802816 | bytes 56969328 | solution.py:119
  161.4 2.8 %constant_dynamic-slice_fusion = (bf16[512,1024]{0,1:T(8,128)(2,1)S(1)}, bf16[512,1024]{0,1:T(8,128)(2,1)S(1)}) fusion(bf16[2048,1024]{0,1:T(8,128)(2,1)} %get-tuple-element.657, s32[]{:T(128)S(6)} %select_n.35, bf16[2048,1024]{0,1:T(8,128)(2,1)} %get-tuple-element.651), kind=kLoop, calls=%fused_computation.19 | loop fusion | bytes 4194308 | tf_op jit(solution)/shard_map/while/body/eval_jaxpr/while/body/eval_jaxpr/cond/branch_1_fun/dynamic_slice | solution.py:89
  164.2 1.4 fusion.11
  165.5 2.7 %fusion.18 = (f32[8,512]{1,0:T(8,128)S(1)}, f32[8,512,512]{1,2,0:T(8,128)S(1)}) fusion(f32[512,512,8]{1,0,2:T(8,128)S(1)} %fusion.11, bf16[512,8,128]{0,2,1:T(8,128)(2,1)S(1)} %bitcast.48, bf16[512,8,128]{2,0,1:T(8,128)(2,1)S(1)} %get-tuple-element.652, pred[512,512]{0,1:T(8,128)(4,1)S(1)} %compare_and_fusion), kind=kOutput, calls=%fused_computation.36 | convolution fusion | flops 545255424 | bytes 19152896 | tf_op jit(solution)/shard_map/while/body/eval_jaxpr/while/body/eval_jaxpr/cond/branch_1_fun/ihd,jhd->hij/dot_general | solution.py:94
  168.2 2.0 bitcast_add_fusion.1
  170.2 1.2 fusion.5
  172.2 1.0 constant_dynamic-update-slice_fusion.2
  173.3 0.6 dynamic_slice.62
  174.6 1.9 constant_dynamic-slice_fusion.7
  176.5 1.3 constant_dynamic-slice_fusion.6
  177.9 0.7 copy.74
  178.8 30.3 %while.56 = (s32[]{:T(128)}, f32[8,512]{1,0:T(8,128)S(1)}, f32[8,512]{1,0:T(8,128)S(1)}, f32[512,8,128]{0,2,1:T(8,128)S(1)}, s32[]{:T(128)}, /*index=5*/s32[2048...) while((s32[]{:T(128)}, f32[8,512]{1,0:T(8,128)S(1)}, ...), condition=%wide.region_8.8_spmd.clone, body=%wide.region_3.7_spmd.clone.sunk | while | flops 1360802816 | bytes 56971772 | solution.py:126
  179.5 0.7 dynamic_slice.64
  182.7 0.7 dynamic_slice.64
  185.2 10.4 %conditional.3 = ((f32[8,512]{1,0:T(8,128)S(1)}, f32[8,512]{1,0:T(8,128)S(1)}, f32[512,8,128]{0,2,1:T(8,128)S(1)})) conditional(s32[]{:T(128)} %bitcast.46, (f32[8,512]{1,0:T(8,128)S(1)}, f32[8,512]{1,0:T(8,128)S(1)}, f32[512,8,128]{0,2,1:T(8,128)S(1)}) %tuple.116, (s32[512]{0:T(512)S(1)}, s32[]{:T(128)}, s32[2048]{0:T(1024)S(1)}, s32[]{:T(128)}, ...), branch_computations={%region_4.3_spmd, %region_5.6_spmd} | conditional | flops 1360802816 | bytes 56969328 | solution.py:119
  185.7 2.8 %constant_dynamic-slice_fusion = (bf16[512,1024]{0,1:T(8,128)(2,1)S(1)}, bf16[512,1024]{0,1:T(8,128)(2,1)S(1)}) fusion(bf16[2048,1024]{0,1:T(8,128)(2,1)} %get-tuple-element.657, s32[]{:T(128)S(6)} %select_n.35, bf16[2048,1024]{0,1:T(8,128)(2,1)} %get-tuple-element.651), kind=kLoop, calls=%fused_computation.19 | loop fusion | bytes 4194308 | tf_op jit(solution)/shard_map/while/body/eval_jaxpr/while/body/eval_jaxpr/cond/branch_1_fun/dynamic_slice | solution.py:89
  188.5 1.4 fusion.11
  189.8 2.7 %fusion.18 = (f32[8,512]{1,0:T(8,128)S(1)}, f32[8,512,512]{1,2,0:T(8,128)S(1)}) fusion(f32[512,512,8]{1,0,2:T(8,128)S(1)} %fusion.11, bf16[512,8,128]{0,2,1:T(8,128)(2,1)S(1)} %bitcast.48, bf16[512,8,128]{2,0,1:T(8,128)(2,1)S(1)} %get-tuple-element.652, pred[512,512]{0,1:T(8,128)(4,1)S(1)} %compare_and_fusion), kind=kOutput, calls=%fused_computation.36 | convolution fusion | flops 545255424 | bytes 19152896 | tf_op jit(solution)/shard_map/while/body/eval_jaxpr/while/body/eval_jaxpr/cond/branch_1_fun/ihd,jhd->hij/dot_general | solution.py:94
  192.5 2.0 bitcast_add_fusion.1
  194.5 1.2 fusion.5
  196.3 0.7 dynamic_slice.64
  198.9 10.3 %conditional.3 = ((f32[8,512]{1,0:T(8,128)S(1)}, f32[8,512]{1,0:T(8,128)S(1)}, f32[512,8,128]{0,2,1:T(8,128)S(1)})) conditional(s32[]{:T(128)} %bitcast.46, (f32[8,512]{1,0:T(8,128)S(1)}, f32[8,512]{1,0:T(8,128)S(1)}, f32[512,8,128]{0,2,1:T(8,128)S(1)}) %tuple.116, (s32[512]{0:T(512)S(1)}, s32[]{:T(128)}, s32[2048]{0:T(1024)S(1)}, s32[]{:T(128)}, ...), branch_computations={%region_4.3_spmd, %region_5.6_spmd} | conditional | flops 1360802816 | bytes 56969328 | solution.py:119
  199.3 2.6 %constant_dynamic-slice_fusion = (bf16[512,1024]{0,1:T(8,128)(2,1)S(1)}, bf16[512,1024]{0,1:T(8,128)(2,1)S(1)}) fusion(bf16[2048,1024]{0,1:T(8,128)(2,1)} %get-tuple-element.657, s32[]{:T(128)S(6)} %select_n.35, bf16[2048,1024]{0,1:T(8,128)(2,1)} %get-tuple-element.651), kind=kLoop, calls=%fused_computation.19 | loop fusion | bytes 4194308 | tf_op jit(solution)/shard_map/while/body/eval_jaxpr/while/body/eval_jaxpr/cond/branch_1_fun/dynamic_slice | solution.py:89
  201.9 1.4 fusion.11
  203.3 2.7 %fusion.18 = (f32[8,512]{1,0:T(8,128)S(1)}, f32[8,512,512]{1,2,0:T(8,128)S(1)}) fusion(f32[512,512,8]{1,0,2:T(8,128)S(1)} %fusion.11, bf16[512,8,128]{0,2,1:T(8,128)(2,1)S(1)} %bitcast.48, bf16[512,8,128]{2,0,1:T(8,128)(2,1)S(1)} %get-tuple-element.652, pred[512,512]{0,1:T(8,128)(4,1)S(1)} %compare_and_fusion), kind=kOutput, calls=%fused_computation.36 | convolution fusion | flops 545255424 | bytes 19152896 | tf_op jit(solution)/shard_map/while/body/eval_jaxpr/while/body/eval_jaxpr/cond/branch_1_fun/ihd,jhd->hij/dot_general | solution.py:94
  206.0 2.0 bitcast_add_fusion.1
  208.0 1.2 fusion.5
  210.0 1.0 constant_dynamic-update-slice_fusion.2
  211.0 31.5 %all_to_all.34 = bf16[8,128,1024]{2,1,0:T(8,128)(2,1)S(1)} all-to-all(bf16[8,128,1024]{2,1,0:T(8,128)(2,1)} %bitcast.55), channel_id=1, replica_groups=mesh['seq_0'=8,'seq_1'=4,'head'=8] {'head'}, dimensions={0} | all-to-all | bytes 4194304 | tf_op jit(solution)/shard_map/all_to_all | solution.py:132
  242.5 2.4 copy.66
  244.9 4.1 %copy.67 = bf16[128,8192]{1,0:T(8,128)(2,1)} copy(bf16[128,8192]{0,1:T(8,128)(2,1)} %bitcast.54) | data formatting | bytes 4194304 | tf_op jit(solution)/shard_map/all_to_all | solution.py:132
  (82 shorter events, 8.6 us)
Async XLA Ops:
  6.5 37.6 %all-gather.4.cloned.1.call-start = ((), (), s32[]{:S(2)}) async-start(), calls=%async_computation.2 | async-start | bytes 1327104 | tf_op jit(solution)/shard_map/all_gather | solution.py:21
  9.0 81.8 %all-gather.6.cloned.1.call-start = ((), (), s32[]{:S(2)}) async-start(), calls=%async_computation.3 | async-start | bytes 1179648 | tf_op jit(solution)/shard_map/all_gather | solution.py:37
  27.0 4.4 %copy-start.1 = (bf16[16,1024]{1,0:T(8,128)(2,1)S(1)}, bf16[16,1024]{1,0:T(8,128)(2,1)}, u32[]{:S(2)}) copy-start(bf16[16,1024]{1,0:T(8,128)(2,1)} %param.16) | copy-start | bytes 98308
  27.0 22.3 %copy-start.2 = (s32[128]{0:T(128)S(1)}, s32[128]{0:T(128)}, u32[]{:S(2)}) copy-start(s32[128]{0:T(128)} %param.17) | copy-start | bytes 1540
  27.0 47.8 %all-to-all-start = ((bf16[128,8,1536]{0,2,1:T(8,128)(2,1)}), bf16[128,8,1536]{0,2,1:T(8,128)(2,1)S(1)}, u32[]{:S(2)}, u32[]{:S(2)}) async-start(bf16[128,8,1536]{0,2,1:T(8,128)(2,1)} %bitcast.52), calls=%async_computation | async-start | bytes 6291456 | tf_op jit(solution)/shard_map/all_to_all | solution.py:58
  31.3 91.2 %all-gather.8.cloned.1.call-start = ((), (), s32[]{:S(2)}) async-start(), calls=%async_computation.4 | async-start | bytes 1179648 | tf_op jit(solution)/shard_map/all_gather | solution.py:37
  46.5 44.2 %collective-permute-start = (bf16[1024,512]{0,1:T(8,128)(2,1)}, bf16[1024,512]{0,1:T(8,128)(2,1)}, u32[]{:S(2)}, u32[]{:S(2)}) collective-permute-start(bf16[1024,512]{0,1:T(8,128)(2,1)} %slice.39), channel_id=1, source_target_pairs={{0,8},{8,16},{16,24},{24,32},{32,40},{40,48},{48,56},{56,64},{64,7... | collective-permute-start | bytes 3145736 | tf_op jit(solution)/shard_map/ppermute | solution.py:31
  51.2 23.5 %collective-permute-start.1 = (bf16[1024,64]{0,1:T(8,128)(2,1)S(1)}, bf16[1024,64]{0,1:T(8,128)(2,1)S(1)}, u32[]{:S(2)}, u32[]{:S(2)}) collective-permute-start(bf16[1024,64]{0,1:T(8,128)(2,1)S(1)} %slice.40), channel_id=1, source_target_pairs={{0,8},{8,16},{16,24},{24,32},{32,40},{40,48},{48,56},{56,64},{64,7... | collective-permute-start | bytes 393224 | tf_op jit(solution)/shard_map/ppermute | solution.py:31
  147.3 3.2 %copy-start = (bf16[512,8,64]{0,2,1:T(8,128)(2,1)S(1)}, bf16[512,8,64]{0,2,1:T(8,128)(2,1)}, u32[]{:S(2)}) copy-start(bf16[512,8,64]{0,2,1:T(8,128)(2,1)} %get-tuple-element.654) | copy-start | bytes 1572868 | tf_op jit(solution)/shard_map/while/body/eval_jaxpr/while/body/eval_jaxpr/cond
  161.0 3.2 %copy-start = (bf16[512,8,64]{0,2,1:T(8,128)(2,1)S(1)}, bf16[512,8,64]{0,2,1:T(8,128)(2,1)}, u32[]{:S(2)}) copy-start(bf16[512,8,64]{0,2,1:T(8,128)(2,1)} %get-tuple-element.654) | copy-start | bytes 1572868 | tf_op jit(solution)/shard_map/while/body/eval_jaxpr/while/body/eval_jaxpr/cond
  185.3 3.2 %copy-start = (bf16[512,8,64]{0,2,1:T(8,128)(2,1)S(1)}, bf16[512,8,64]{0,2,1:T(8,128)(2,1)}, u32[]{:S(2)}) copy-start(bf16[512,8,64]{0,2,1:T(8,128)(2,1)} %get-tuple-element.654) | copy-start | bytes 1572868 | tf_op jit(solution)/shard_map/while/body/eval_jaxpr/while/body/eval_jaxpr/cond
  198.9 3.0 %copy-start = (bf16[512,8,64]{0,2,1:T(8,128)(2,1)S(1)}, bf16[512,8,64]{0,2,1:T(8,128)(2,1)}, u32[]{:S(2)}) copy-start(bf16[512,8,64]{0,2,1:T(8,128)(2,1)} %get-tuple-element.654) | copy-start | bytes 1572868 | tf_op jit(solution)/shard_map/while/body/eval_jaxpr/while/body/eval_jaxpr/cond
Sparse Core Ops, SparseCore 0:
  9.2 30.8 all-gather.3
  41.8 40.7 all-gather.5
  84.4 38.1 all-gather.7
where the time goes:
time: 257 us; the launch traced here: 255 us
  local copies, waits for them, and re-layouts  76.2 us (30%)
  blocking collectives  57.4 us (22%)
  waiting for transfers between devices  38.8 us (15%)
  matrix products  36.5 us (14%)
  loops' own time  13.6 us (5%)
  between operations  13.2 us (5%)
  starting transfers between devices  10.9 us (4%)
  other arithmetic  8.73 us (3%)
    all_to_all x1, blocking collectives, shards(): lax.all_to_all(attended, 'head', split_axis=0, concat_axis=1, tiled=True)  31.5 us
    all_gather x2, blocking collectives, gathered_by_axis(): nearer = lax.all_gather(shard, axes[-1], axis=dim, tiled=True)  26 us
    ppermute x2, waiting for transfers between devices, shifted(): lax.ppermute(value, axis, [(source, source + steps) for source in range(f...  19.7 us
    all_gather x2, waiting for transfers between devices, gathered_by_axis(): nearer = lax.all_gather(shard, axes[-1], axis=dim, tiled=True)  19 us
    while x2, local copies, waits for them, and re-layouts, shards(): lax.map(one_block, jnp.arange(group_rows // block_rows, dtype=jnp.int32))  13 us
    another operation x2, loops' own time, one_block(): lax.fori_loop(0, key_blocks, visit, start_state)  11.8 us
    dynamic_slice x4, local copies, waits for them, and re-layouts, attend(): lax.dynamic_slice_in_dim(values_all, k_start, block_rows, 0)  11.1 us
    dot_general x4, matrix products, attend(): jnp.einsum('ihd,jhd->hij', q_nope, k_nope, preferred_element_type=jnp.flo...  10.7 us
  transfers between devices with their start and end apart: 6, of which 2 were waited for; matrix products, arithmetic and copies ran while one was open for 15% of the time, Pallas kernels for 0%

commit v1 on v0

v1 whole, which is shorter than its diff:
```python
import functools
import math

import jax
import jax.numpy as jnp
from jax import lax
from jax.experimental import pallas as pl
from jax.experimental.pallas import tpu as pltpu
from jax.sharding import Mesh
from jax.sharding import PartitionSpec as P

NOPE = 128
ROPE = 64
VDIM = 128
PAIR = 384
NX, NY, NZ, NC = 4, 4, 8, 2
HEADS_EACH = 8
SLAB = 16
TOK = 128
KEYS = 6 * TOK
WIN = 5 * TOK
LATENT = 512
LOWEST = -1e30
EXP_SCALE = math.log2(math.e) / math.sqrt(NOPE + ROPE)
SIZES = {"x": NX, "y": NY, "z": NZ}

X_LAST = (0, 1, 2)
Y_LAST = (3, 4, 5)
Z_LAST = (6, 7)
FULL = {"x": (0, NX), "y": (0, NY), "z": (0, NZ)}


class Transfer:
    def __init__(self, name, kind, where, target, deps, link, size, hops=1):
        self.name, self.kind, self.where, self.target = name, kind, where, target
        self.deps, self.link, self.size, self.hops = list(deps), link, size, hops


def weight_transfers():
    out = []

    def own(**over):
        spot = {"x": ("at", 0), "y": ("at", 0), "z": ("at", 0)}
        spot.update(over)
        return spot

    def size_of(spot, heads):
        count = 1
        for axis in "xyz":
            what = spot[axis]
            count *= 1 if what[0] == "at" else what[1]
        return count * heads[1] * SLAB * 2 * NOPE * 2

    def add(name, spot, heads, target, deps, hops=1):
        axis, step = target
        link = axis + ("+" if step > 0 else "-")
        out.append(Transfer(name, "w", (spot, heads), target, deps, link, size_of(spot, heads), hops))
        return name

    def direct(tag, axis, heads, deps):
        got = []
        n = SIZES[axis]
        for step in [s for d in range(1, n // 2 + 1) for s in ((d, -d) if 2 * d < n else (d,))]:
            got.append(add(f"{tag}.{axis}{step}", own(), heads, (axis, step), deps, abs(step)))
        return got

    def ring(tag, axis, spot, heads, deps, half_axis):
        n = SIZES[axis]
        got = {0: list(deps)}
        lo = spot[half_axis][1] // 2
        for sign in (1, -1):
            last = list(deps)
            for k in range(1, n // 2 + 1):
                piece = dict(spot)
                piece[axis] = ("at", -sign * (k - 1))
                if k == n // 2:
                    piece[half_axis] = (0 if sign > 0 else lo, lo)
                name = add(f"{tag}.{axis}{'+' if sign > 0 else '-'}{k}", piece, heads, (axis, sign), last)
                last = [name]
                if k == n // 2:
                    got.setdefault(n // 2, []).append(name)
                else:
                    got[-sign * k] = [name]
        return got

    local = ["load"]
    ready = {}
    first = {}
    for i in range(3):
        for h in (X_LAST[i], Y_LAST[i]):
            first[h] = direct(f"f{h}", "z", (h, 1), local)
        if i == 0:
            zl = (Z_LAST[0], len(Z_LAST))
            c1 = direct("cx", "x", zl, local)
            c2 = ring("cy", "y", own(x=FULL["x"]), zl, c1 + local, "x")
            c_all = sum(c2.values(), [])
    for i in range(3):
        h = X_LAST[i]
        got = ring(f"a{h}", "y", own(z=FULL["z"]), (h, 1), first[h] + local, "z")
        all_y = sorted(set(sum(got.values(), [])))
        got = ring(f"a{h}", "x", own(z=FULL["z"], y=FULL["y"]), (h, 1), all_y, "z")
        for dx, names in got.items():
            ready[("a", h, dx)] = sorted(set(names))
        h = Y_LAST[i]
        got = ring(f"b{h}", "x", own(z=FULL["z"]), (h, 1), first[h] + local, "z")
        all_x = sorted(set(sum(got.values(), [])))
        got = ring(f"b{h}", "y", own(z=FULL["z"], x=FULL["x"]), (h, 1), all_x, "z")
        ready[("b", h, None)] = sorted(set(sum(got.values(), [])))
        if i < 2:
            h = Z_LAST[i]
            got = ring(f"c{h}", "z", own(x=FULL["x"], y=FULL["y"]), (h, 1), sorted(set(c_all)), "x")
            ready[("c", h, None)] = sorted(set(sum(got.values(), [])))
    return out, ready


def other_transfers():
    lat = TOK * (LATENT + 128) * 2
    q = TOK * 4 * PAIR * 2
    out = [
        Transfer("lat.next", "lat", ("in", 2), "next", [], "x+", lat),
        Transfer("lat.core", "lat", ("in", 4), "core", [], "c", lat),
        Transfer("lat.next2", "lat", (2, 0), "next", ["lat.next"], "x+", lat),
        Transfer("lat.core1", "lat", (2, 2), "core", ["lat.next"], "c", lat),
        Transfer("lat.core2", "lat", (0, 0), "core", ["lat.next2"], "c", lat),
    ]
    for x in range(NX):
        out.append(Transfer(f"q{x}", "q", x, "core", [], "c", q))
    lat_names = [t.name for t in out if t.kind == "lat"]
    return out, lat_names


def plan(transfers, units, head_us, rate=46.6e3, d2d=300e3):
    by_name = {t.name: t for t in transfers}
    free, arrive, sent = {}, {}, set()
    order, seen = [], set()
    now = 0.0

    def issue():
        for t in transfers:
            if t.name not in sent and all(d in seen for d in t.deps):
                begin = max(now, free.get(t.link, 0.0))
                free[t.link] = begin + t.size * t.hops / (d2d if t.link == "c" else rate)
                arrive[t.name] = free[t.link] + 1.0 + 0.75 * t.hops
                sent.add(t.name)
                order.append(("send", t.name))

    order.append(("load", None))
    seen.add("load")
    issue()
    todo = list(units)
    while todo or len(seen) <= len(transfers):
        waiting = sorted((when, name) for name, when in arrive.items() if name not in seen)
        unit = next((u for u in todo if all(d in seen for d in u[1])), None)
        if waiting and (waiting[0][0] <= now or unit is None):
            when, name = waiting[0]
            now = max(now, when)
            seen.add(name)
            order.append(("wait", name))
            issue()
        else:
            todo.remove(unit)
            order.append(("head", unit[0]))
            now += head_us * unit[2]
    order.append(("end", now))
    return order


def head_units(ready, after):
    units = []
    for (kind, h, dx), names in ready.items():
        units.append(((kind, h, dx), names + after, 1 if kind == "a" else NX))
    return units


def kernel(order, index, parts, q_ref, lat_ref, rope_ref, kw_ref, vw_ref, len_ref, out_ref,
           wbuf, qb, latb, ropeb, rope2, kext0, kext1, vbuf, bias, outb,
           send_sem, recv_sem, load_sem, out_sem, give_sem, take_sem):
    me = {a: lax.axis_index(a) for a in "xyz"}
    core = lax.axis_index("c")
    other = 1 - core
    chip = (me["z"] * NY + me["y"]) * NX + me["x"]

    def at(axis, step):
        return lax.rem(me[axis] + step + 2 * SIZES[axis], SIZES[axis])

    def chip_id(step):
        b = lax.rem(chip + step + NX * NY * NZ, NX * NY * NZ)
        return {"z": b // (NY * NX), "y": lax.rem(b // NX, NY), "x": lax.rem(b, NX)}

    def device(target):
        if target == "core":
            return {"c": other}
        if target == "next":
            return chip_id(1)
        axis, step = target
        return {axis: at(axis, step)}

    barrier = pltpu.get_barrier_semaphore()
    greeted = [{"c": other}, chip_id(1), chip_id(-1)]
    greeted += [{"x": at("x", s)} for s in range(1, NX)]
    greeted += [{"y": at("y", s)} for s in range(1, NY)]
    greeted += [{"z": at("z", s)} for s in range(1, NZ)]
    for d in greeted:
        pl.semaphore_signal(barrier, inc=1, device_id=d, device_id_type=pl.DeviceIdType.MESH)

    loads = []

    def load(src, dst):
        c = pltpu.make_async_copy(src, dst, load_sem.at[len(loads)])
        c.start()
        loads.append(c)

    for h in range(HEADS_EACH):
        for part, ref in enumerate((kw_ref, vw_ref)):
            load(ref.at[:, pl.ds(h * NOPE, NOPE)],
                 wbuf.at[me["x"], h, me["z"], me["y"], :, pl.ds(part * NOPE, NOPE)])
    early = len(loads)
    load(lat_ref, latb.at[4 + core])
    load(rope_ref, ropeb.at[4 + core])
    for x in range(NX):
        start = pl.multiple_of((2 * x + core) * 4 * PAIR, 128)
        load(q_ref.at[:, pl.ds(start, 4 * PAIR)], qb.at[core, x])

    def weight_spot(where):
        spot, heads = where
        idx = {}
        for axis in "xyz":
            what = spot[axis]
            idx[axis] = at(axis, what[1]) if what[0] == "at" else pl.ds(what[0], what[1])
        return wbuf.at[idx["x"], pl.ds(heads[0], heads[1]), idx["z"], idx["y"]]

    def copies(name):
        t = parts[name]
        k = index[name]
        if t.kind == "w":
            pairs = [(weight_spot(t.where), weight_spot(t.where))]
        elif t.kind == "lat":
            src, dst = t.where
            if src == "in":
                pairs = [(lat_ref, latb.at[dst + core]), (rope_ref, ropeb.at[dst + core])]
            else:
                pairs = [(latb.at[src + core], latb.at[dst + core]),
                         (ropeb.at[src + core], ropeb.at[dst + core])]
        else:
            start = pl.multiple_of((2 * t.where + other) * 4 * PAIR, 128)
            pairs = [(q_ref.at[:, pl.ds(start, 4 * PAIR)], qb.at[core, t.where])]
        return [
            pltpu.make_async_remote_copy(
                src_ref=s, dst_ref=d, send_sem=send_sem.at[k + i], recv_sem=recv_sem.at[k + i],
                device_id=device(t.target), device_id_type=pl.DeviceIdType.MESH,
            )
            for i, (s, d) in enumerate(pairs)
        ]

    lens = len_ref[...].astype(jnp.float32)
    rows = lax.broadcasted_iota(jnp.int32, (128, 128), 0)
    cols = lax.broadcasted_iota(jnp.int32, (128, 128), 1)
    as_rows = jnp.broadcast_to(lens, (128, 128))
    as_column = jnp.sum(jnp.where(rows == cols, as_rows, 0.0), axis=1, keepdims=True)
    starts = jnp.sum(jnp.where(rows < cols, as_column, 0.0), axis=0, keepdims=True)
    for half in range(2):
        base = chip * (NC * TOK) + half * TOK
        q_pos = (base + lax.broadcasted_iota(jnp.int32, (TOK, 128), 0)).astype(jnp.float32)
        started = jnp.where(starts <= q_pos, starts, 0.0)
        q_start = jnp.max(started, axis=1, keepdims=True)
        k_pos = (base - 4 * TOK + lax.broadcasted_iota(jnp.int32, (TOK, WIN), 1)).astype(jnp.float32)
        q_row = (base + lax.broadcasted_iota(jnp.int32, (TOK, WIN), 0)).astype(jnp.float32)
        seen = (k_pos >= q_start) & (k_pos <= q_row)
        bias[half] = jnp.where(seen, 0.0, LOWEST)

    lane = lax.broadcasted_iota(jnp.int32, (KEYS, 128), 1)

    def prepare():
        r = ropeb[...].reshape(KEYS, ROPE).astype(jnp.float32)
        r = jnp.concatenate([r, r], axis=1)
        rope2[...] = r.astype(jnp.bfloat16)
        kext0[:, NOPE:] = jnp.where(lane < ROPE, r, 0.0).astype(jnp.bfloat16)

    def one_head(x, h):
        w = wbuf[x, h].reshape(LATENT, 2 * NOPE)
        kv = jnp.dot(latb[...].reshape(KEYS, LATENT), w, preferred_element_type=jnp.float32)
        keys = kv[:, :NOPE]
        vbuf[...] = kv[:, NOPE:].astype(jnp.bfloat16)
        if h % 2 == 0:
            kext = kext0
            kext0[:, :NOPE] = keys.astype(jnp.bfloat16)
        else:
            kext = kext1
            turned = pltpu.roll(keys, 64, 1)
            kext1[:, :NOPE] = jnp.where(lane < 64, 0.0, turned).astype(jnp.bfloat16)
            kext1[:, NOPE:] = jnp.where(lane < 64, turned.astype(jnp.bfloat16), rope2[...])
        column = (h // 2) * PAIR + (h % 2) * 128
        for half in range(2):
            q = qb[half, x, :, pl.ds(column, 256)]
            s = lax.dot_general(q, kext[pl.ds(half * TOK, WIN), :], (((1,), (1,)), ((), ())),
                                preferred_element_type=jnp.float32)
            s = s + bias[half]
            peak = jnp.max(s, axis=1, keepdims=True)
            expo = jnp.exp2((s - peak) * EXP_SCALE)
            total = jnp.sum(expo, axis=1, keepdims=True)
            mixed = jnp.dot(expo.astype(jnp.bfloat16), vbuf[pl.ds(half * TOK, WIN), :],
                            preferred_element_type=jnp.float32)
            outb[half, x, h] = (mixed / total).astype(jnp.bfloat16)

    def out_copies(x, h):
        mine = pl.multiple_of(((2 * x + core) * HEADS_EACH + h) * VDIM, VDIM)
        slot = x * HEADS_EACH + h
        spot = out_ref.at[:, pl.ds(mine, VDIM)]
        local = pltpu.make_async_copy(outb.at[core, x, h], spot, out_sem.at[slot])
        away = pltpu.make_async_remote_copy(
            src_ref=outb.at[other, x, h], dst_ref=spot,
            send_sem=give_sem.at[slot], recv_sem=take_sem.at[slot],
            device_id={"c": other}, device_id_type=pl.DeviceIdType.MESH,
        )
        return local, away

    def put_out(done):
        for x, h in done:
            for c in out_copies(x, h):
                c.start()

    pl.semaphore_wait(barrier, len(greeted))
    sent, finished, prepared, loaded = [], [], False, False
    for what, name in order:
        if what == "load":
            for c in loads[:early]:
                c.wait()
        elif what == "send":
            for c in copies(name):
                c.start()
            sent.append(name)
        elif what == "wait":
            for c in copies(name):
                c.wait_recv()
        elif what == "head":
            if not prepared:
                for c in loads[early:]:
                    c.wait()
                prepare()
                prepared = True
            kind, h, dx = name
            if kind == "a":
                x = at("x", dx)
                one_head(x, h)
                done = [(x, h)]
            else:
                lax.fori_loop(0, NX, lambda x, _: (one_head(x, h), 0)[1], 0)
                done = [(x, h) for x in range(NX)]
            put_out(finished)
            finished = done
            all_done = None
    put_out(finished)
    for name in sent:
        for c in copies(name):
            c.wait_send()
    for x in range(NX):
        for h in range(HEADS_EACH):
            local, away = out_copies(x, h)
            local.wait()
            away.wait()


def shards(queries, latent, rope_keys, key_weight, value_weight, doc_lengths):
    weights, ready = weight_transfers()
    rest, lat_names = other_transfers()
    lats = [t for t in rest if t.kind == "lat"]
    qs = [t for t in rest if t.kind == "q"]
    transfers = lats[:2] + weights + lats[2:] + qs
    after = lat_names + [t.name for t in qs] + ["load"]
    order = plan(transfers, head_units(ready, after), HEAD_US)[:-1]
    index, at = {}, 0
    for t in transfers:
        index[t.name] = at
        at += 2 if t.kind == "lat" else 1
    parts = {t.name: t for t in transfers}
    hbm = pl.BlockSpec(memory_space=pl.ANY)
    bf = jnp.bfloat16
    return pl.pallas_call(
        functools.partial(kernel, order, index, parts),
        out_shape=jax.ShapeDtypeStruct((TOK, 64 * VDIM), bf),
        in_specs=[hbm] * 5 + [pl.BlockSpec(memory_space=pltpu.VMEM)],
        out_specs=hbm,
        scratch_shapes=[
            pltpu.VMEM((NX, HEADS_EACH, NZ, NY, SLAB, 2 * NOPE), bf),
            pltpu.VMEM((NC, NX, TOK, 4 * PAIR), bf),
            pltpu.VMEM((6, TOK, LATENT), bf),
            pltpu.VMEM((6, TOK, ROPE), bf),
            pltpu.VMEM((KEYS, 128), bf),
            pltpu.VMEM((KEYS, 256), bf),
            pltpu.VMEM((KEYS, 256), bf),
            pltpu.VMEM((KEYS, VDIM), bf),
            pltpu.VMEM((NC, TOK, WIN), jnp.float32),
            pltpu.VMEM((NC, NX, HEADS_EACH, TOK, VDIM), bf),
            pltpu.SemaphoreType.DMA((at,)),
            pltpu.SemaphoreType.DMA((at,)),
            pltpu.SemaphoreType.DMA((2 * HEADS_EACH + 2 + NX,)),
            pltpu.SemaphoreType.DMA((NX * HEADS_EACH,)),
            pltpu.SemaphoreType.DMA((NX * HEADS_EACH,)),
            pltpu.SemaphoreType.DMA((NX * HEADS_EACH,)),
        ],
        compiler_params=pltpu.CompilerParams(
            collective_id=0, has_side_effects=True, vmem_limit_bytes=56 * 2**20
        ),
    )(queries, latent, rope_keys, key_weight, value_weight, doc_lengths.reshape(1, -1))


HEAD_US = 0.75


def solution(mesh):
    torus = Mesh(mesh.devices.reshape(NZ, NY, NX, NC), ("z", "y", "x", "c"))
    rows = P(("z", "y", "x", "c"), None)
    weight = P(("z", "y"), ("x", "c"))
    return jax.shard_map(
        shards, mesh=torus, in_specs=(rows, rows, rows, weight, weight, P()), out_specs=rows,
        check_vma=False,
    )
```

time: 257 us -> 103 us (0.40)
  the two profiles are of different devices: /device:TPU:8 before, /device:TPU:1 now
where the time goes in v1:
time: 103 us
  Pallas kernels  98.2 us (95%)
  local copies, waits for them, and re-layouts  4.53 us (4%)
    pallas_call x1, Pallas kernels, shards(): pl.pallas_call(functools.partial(kernel, order, index, parts), out_shape=...  98.2 us
    unnamed x2, local copies, waits for them, and re-layouts  4.53 us

profile of v1, /device:TPU:1, one launch (start us, length us, event | category | flops | bytes accessed | tf_op | source)
XLA Modules:
  0.0 102.8 jit_solution(7539679234926390013)
XLA Ops:
  0.0 1.4 %copy.7.rope_ref = bf16[128,64]{1,0:T(8,128)(2,1)} copy(bf16[128,64]{0,1:T(8,128)(2,1)} %param.8) | data formatting | bytes 32768 | tf_op args[2]
  1.4 98.2 %shard_map.64 = bf16[128,8192]{1,0:T(8,128)(2,1)} custom-call(bf16[128,12288]{1,0:T(8,128)(2,1)} %q_ref.1, bf16[128,512]{1,0:T(8,128)(2,1)} %lat_ref.1, bf16[128,64]{1,0:T(8,128)(2,1)} %copy.7.rope_ref, bf16[16,1024]{1,0:T(8,128)(2,1)} %kw_ref.1, bf16[16,1024]{1,0:T(8,128)(2,1)} %vw_ref.1, s32[1,128]{1,0:T(1,128)} %bitcast.1), custom_call_target="tpu_custom_call" | custom-call | tf_op jit(solution)/shard_map/pallas_call | solution.py:378
  99.7 3.1 %copy.9 = bf16[128,8192]{1,0:T(8,128)(2,1)} copy(bf16[128,8192]{1,0:T(8,128)(2,1)} %shard_map.64) | data formatting | bytes 4194304

commit v2 on v1

v2 whole, which is shorter than its diff:
```python
import functools
import math

import jax
import jax.numpy as jnp
from jax import lax
from jax.experimental import pallas as pl
from jax.experimental.pallas import tpu as pltpu
from jax.sharding import Mesh
from jax.sharding import PartitionSpec as P

NOPE = 128
ROPE = 64
VDIM = 128
PAIR = 384
NX, NY, NZ, NC = 4, 4, 8, 2
HEADS_EACH = 8
SLAB = 16
TOK = 128
KEYS = 6 * TOK
WIN = 5 * TOK
LATENT = 512
LOWEST = -1e30
EXP_SCALE = math.log2(math.e) / math.sqrt(NOPE + ROPE)
SIZES = {"x": NX, "y": NY, "z": NZ}
FULL = {"x": (0, NX), "y": (0, NY), "z": (0, NZ)}

X_LAST = (0, 1, 2)
Y_LAST = (5, 4, 3)
Z_LAST = (6, 7)
LATER = (1, 4)
FINE = (True, False, False)
X_FORWARD = 3
DEPTH = 4.0
UNIT_US = {1: 1.1, 2: 1.5, 4: 3.0}
NT = (((1,), (1,)), ((), ()))
TN = (((0,), (0,)), ((), ()))


def PRIORITY(t, reach):
    return 0


class Transfer:
    def __init__(self, name, kind, where, target, deps, link, size, hops=1):
        self.name, self.kind, self.where, self.target = name, kind, where, target
        self.deps, self.link, self.size, self.hops = list(deps), link, size, hops


def weight_transfers():
    out, ready = [], {}

    def own(**over):
        spot = {"x": ("at", 0), "y": ("at", 0), "z": ("at", 0)}
        spot.update(over)
        return spot

    def add(name, spot, heads, target, deps, hops=1):
        axis, step = target
        count = heads[1]
        for a in "xyz":
            count *= 1 if spot[a][0] == "at" else spot[a][1]
        link = axis + ("+" if step > 0 else "-")
        size = count * SLAB * 2 * NOPE * 2
        out.append(Transfer(name, "w", (spot, heads), target, deps, link, size, hops))
        return name

    def direct(tag, axis, heads, deps, far=1):
        n = SIZES[axis]
        steps = [s for d in range(1, n // 2) for s in (d, -d)] + [far * (n // 2)]
        return [add(f"{tag}{axis}{s}", own(), heads, (axis, s), deps, abs(s)) for s in steps]

    def ring(tag, axis, spot, heads, deps, half_axis, forward=None):
        n = SIZES[axis]
        got = {0: list(deps)}
        lo, width = heads if half_axis == "h" else spot[half_axis]
        cut = width // 2 if forward is None else forward
        for sign in (1, -1):
            last = list(deps)
            for k in range(1, n // 2 + 1):
                piece, part = dict(spot), heads
                piece[axis] = ("at", -sign * (k - 1))
                if k == n // 2:
                    share = (lo, cut) if sign > 0 else (lo + cut, width - cut)
                    if share[1] == 0:
                        continue
                    if half_axis == "h":
                        part = share
                    else:
                        piece[half_axis] = share
                name = add(f"{tag}{axis}{'+' if sign > 0 else '-'}{k}", piece, part, (axis, sign), last)
                last = [name]
                got.setdefault(n // 2 if k == n // 2 else -sign * k, []).append(name)
        return got

    def last_ring(tag, axis, inner, spot, heads, units, forward=None):
        got = {}
        for offset, deps in units.items():
            piece = dict(spot)
            if offset is None:
                piece[inner] = FULL[inner]
            else:
                piece[inner] = ("at", offset)
            for o, names in ring(f"{tag}u{offset}", axis, piece, heads, deps, "z", forward).items():
                got.setdefault(o, []).extend(names)
        return {o: sorted(set(names)) for o, names in got.items()}

    def whole(units):
        return {None: sorted(set(sum(units.values(), [])))}

    local = ["load"]
    first = {X_LAST[0]: direct("f0", "z", (X_LAST[0], 1), local, 1),
             Y_LAST[0]: direct("f1", "z", (Y_LAST[0], 1), local, -1)}
    zl = (Z_LAST[0], len(Z_LAST))
    c_first = direct("fc", "x", zl, local, -1)
    later = ring("f2", "z", own(), LATER, local, "h")
    later = sorted(set(sum(later.values(), [])))
    for h in X_LAST[1:] + Y_LAST[1:]:
        first[h] = later
    c_units = ring("c", "y", own(x=FULL["x"]), zl, c_first + local, "x")
    c_all = whole(c_units)[None]
    for i in range(3):
        h = X_LAST[i]
        units = ring(f"a{i}", "y", own(z=FULL["z"]), (h, 1), first[h] + local, "z")
        if not FINE[i]:
            units = whole(units)
        got = last_ring(f"a{i}", "x", "y", own(z=FULL["z"]), (h, 1), units, X_FORWARD)
        ready[("a", h, (0,))] = got[0]
        ready[("a", h, (-1, 1))] = sorted(set(got[-1] + got[1]))
        ready[("a", h, (2,))] = got[2]
        h = Y_LAST[i]
        units = ring(f"b{i}", "x", own(z=FULL["z"]), (h, 1), first[h] + local, "z")
        if not FINE[i]:
            units = whole(units)
        got = last_ring(f"b{i}", "y", "x", own(z=FULL["z"]), (h, 1), units)
        ready[("b", h, None)] = sorted(set(sum(got.values(), [])))
        if i < 2:
            h = Z_LAST[i]
            got = ring(f"c{i}", "z", own(x=FULL["x"], y=FULL["y"]), (h, 1), c_all, "x")
            ready[("c", h, None)] = sorted(set(sum(got.values(), [])))
    return out, ready


def other_transfers():
    lat = TOK * (LATENT + 64) * 2
    q = TOK * 4 * PAIR * 2
    out = [
        Transfer("lat.next", "lat", ("in", 2), "next", [], "x+", lat),
        Transfer("lat.core", "lat", ("in", 4), "core", [], "c", lat),
        Transfer("lat.next2", "lat", (2, 0), "next", ["lat.next"], "x+", lat),
        Transfer("lat.core1", "lat", (2, 2), "core", ["lat.next"], "c", lat),
        Transfer("lat.core2", "lat", (0, 0), "core", ["lat.next2"], "c", lat),
    ]
    lat_names = [t.name for t in out]
    for x in range(NX):
        out.append(Transfer(f"q{x}", "q", x, "core", [], "c", q))
    return out, lat_names


def plan(transfers, units, rate=46.6e3, d2d=600e3, depth=4.0):
    by_name = {t.name: t for t in transfers}
    tail = {}
    follow = {}
    for t in transfers:
        for d in t.deps:
            follow.setdefault(d, []).append(t.name)

    def cost(t):
        return t.size * t.hops / (d2d if t.link == "c" else rate)

    def reach(name):
        if name not in tail:
            tail[name] = cost(by_name[name]) + 1.0 + 0.75 * by_name[name].hops + max(
                [reach(f) for f in follow.get(name, [])], default=0.0)
        return tail[name]

    rank = {t.name: (PRIORITY(t, reach(t.name)), i) for i, t in enumerate(transfers)}
    free, arrive, sent = {}, {}, set()
    order, seen = [], set()
    now = 0.0

    def issue():
        for t in sorted(transfers, key=lambda t: rank[t.name]):
            if t.name not in sent and all(d in seen for d in t.deps):
                if free.get(t.link, 0.0) - now > depth:
                    continue
                free[t.link] = max(now, free.get(t.link, 0.0)) + cost(t)
                arrive[t.name] = free[t.link] + 1.0 + 0.75 * t.hops
                sent.add(t.name)
                order.append(("send", t.name))

    order.append(("load", None))
    seen.add("load")
    issue()
    todo = list(units)
    busy = 0.0
    while todo or len(seen) <= len(transfers):
        waiting = sorted((when, name) for name, when in arrive.items() if name not in seen)
        unit = next((u for u in todo if all(d in seen for d in u[1])), None)
        if waiting and (waiting[0][0] <= now or unit is None):
            when, name = waiting[0]
            now = max(now, when)
            seen.add(name)
            order.append(("wait", name))
            issue()
        elif unit is not None:
            todo.remove(unit)
            order.append(("head", unit[0]))
            now += unit[2]
            busy += unit[2]
            issue()
        else:
            now += 0.2
            issue()
    return order, now, max(arrive.values(), default=0), busy


def kernel(order, index, parts, q_ref, lat_ref, rope_ref, kw_ref, vw_ref, len_ref, out_ref,
           wbuf, qb, latb, ropeb, rope2, kexts, vbufs, bias, outb,
           send_sem, recv_sem, load_sem, out_sem, give_sem, take_sem):
    me = {a: lax.axis_index(a) for a in "xyz"}
    core = lax.axis_index("c")
    other = 1 - core
    chip = (me["z"] * NY + me["y"]) * NX + me["x"]

    def at(axis, step):
        return lax.rem(me[axis] + step + 2 * SIZES[axis], SIZES[axis])

    def chip_id(step):
        b = lax.rem(chip + step + NX * NY * NZ, NX * NY * NZ)
        return {"z": b // (NY * NX), "y": lax.rem(b // NX, NY), "x": lax.rem(b, NX)}

    def device(target):
        if target == "core":
            return {"c": other}
        if target == "next":
            return chip_id(1)
        axis, step = target
        return {axis: at(axis, step)}

    barrier = pltpu.get_barrier_semaphore()
    greeted = [{"c": other}, chip_id(1), chip_id(-1)]
    greeted += [{a: at(a, s)} for a in "xyz" for s in range(1, SIZES[a])]
    for d in greeted:
        pl.semaphore_signal(barrier, inc=1, device_id=d, device_id_type=pl.DeviceIdType.MESH)

    loads = []

    def load(src, dst):
        c = pltpu.make_async_copy(src, dst, load_sem.at[len(loads)])
        c.start()
        loads.append(c)

    for h in range(HEADS_EACH):
        for part, ref in enumerate((kw_ref, vw_ref)):
            load(ref.at[:, pl.ds(h * NOPE, NOPE)],
                 wbuf.at[me["x"], h, me["z"], me["y"], :, pl.ds(part * NOPE, NOPE)])
    early = len(loads)
    load(lat_ref, latb.at[4 + core])
    load(rope_ref, ropeb.at[4 + core])
    for x in range(NX):
        start = pl.multiple_of((2 * x + core) * 4 * PAIR, 128)
        load(q_ref.at[:, pl.ds(start, 4 * PAIR)], qb.at[x, core])

    def weight_spot(where):
        spot, heads = where
        idx = {}
        for axis in "xyz":
            what = spot[axis]
            idx[axis] = at(axis, what[1]) if what[0] == "at" else pl.ds(what[0], what[1])
        return wbuf.at[idx["x"], pl.ds(heads[0], heads[1]), idx["z"], idx["y"]]

    def copies(name):
        t = parts[name]
        k = index[name]
        if t.kind == "w":
            pairs = [(weight_spot(t.where), weight_spot(t.where))]
        elif t.kind == "lat":
            src, dst = t.where
            if src == "in":
                pairs = [(lat_ref, latb.at[dst + core]), (rope_ref, ropeb.at[dst + core])]
            else:
                pairs = [(latb.at[src + core], latb.at[dst + core]),
                         (ropeb.at[src + core], ropeb.at[dst + core])]
        else:
            start = pl.multiple_of((2 * t.where + other) * 4 * PAIR, 128)
            pairs = [(q_ref.at[:, pl.ds(start, 4 * PAIR)], qb.at[t.where, core])]
        return [
            pltpu.make_async_remote_copy(
                src_ref=s, dst_ref=d, send_sem=send_sem.at[k + i], recv_sem=recv_sem.at[k + i],
                device_id=device(t.target), device_id_type=pl.DeviceIdType.MESH,
            )
            for i, (s, d) in enumerate(pairs)
        ]

    lane = lax.broadcasted_iota(jnp.int32, (KEYS, 128), 1)

    def make_bias():
        lens = len_ref[...].astype(jnp.float32)
        rows = lax.broadcasted_iota(jnp.int32, (128, 128), 0)
        cols = lax.broadcasted_iota(jnp.int32, (128, 128), 1)
        as_rows = jnp.broadcast_to(lens, (128, 128))
        starts = jnp.sum(jnp.where(cols < rows, as_rows, 0.0), axis=1, keepdims=True)
        for half in range(NC):
            base = chip * (NC * TOK) + half * TOK
            q_pos = (base + cols).astype(jnp.float32)
            started = jnp.where(starts <= q_pos, starts, 0.0)
            q_start = jnp.max(started, axis=0, keepdims=True)
            k_pos = (base - 4 * TOK + lax.broadcasted_iota(jnp.int32, (WIN, TOK), 0)).astype(jnp.float32)
            q_row = (base + lax.broadcasted_iota(jnp.int32, (WIN, TOK), 1)).astype(jnp.float32)
            bias[half] = jnp.where((k_pos >= q_start) & (k_pos <= q_row), 0.0, LOWEST)

    def prepare():
        for s in range(6):
            r = ropeb[s].astype(jnp.float32)
            r = jnp.transpose(jnp.concatenate([r, r], axis=0))
            spot = pl.ds(s * TOK, TOK)
            rope2[spot, :] = r.astype(jnp.bfloat16)
            for slot in range(2):
                kexts[2 * slot, spot, NOPE:] = jnp.where(lane[:TOK] < ROPE, r, 0.0).astype(jnp.bfloat16)

    def project(x, h, slot):
        w = wbuf[x, h].reshape(LATENT, 2 * NOPE)
        kv = jnp.dot(latb[...].reshape(KEYS, LATENT), w, preferred_element_type=jnp.float32)
        keys = kv[:, :NOPE]
        vbufs[slot] = kv[:, NOPE:].astype(jnp.bfloat16)
        if h % 2 == 0:
            kexts[2 * slot, :, :NOPE] = keys.astype(jnp.bfloat16)
        else:
            turned = pltpu.roll(keys, 64, 1)
            kexts[2 * slot + 1, :, :NOPE] = jnp.where(lane < 64, 0.0, turned).astype(jnp.bfloat16)
            kexts[2 * slot + 1, :, NOPE:] = jnp.where(lane < 64, turned.astype(jnp.bfloat16), rope2[...])

    def attend(x, h, slot):
        column = (h // 2) * PAIR + (h % 2) * 128
        q = qb[x, :, :, pl.ds(column, 256)].reshape(NC * TOK, 256)
        scores = lax.dot_general(kexts[2 * slot + h % 2], q, NT, preferred_element_type=jnp.float32)
        for half in range(NC):
            at_keys, at_rows = slice(half * TOK, half * TOK + WIN), slice(half * TOK, half * TOK + TOK)
            s = scores[at_keys, at_rows] + bias[half]
            peak = jnp.max(s, axis=0, keepdims=True)
            expo = jnp.exp2((s - peak) * EXP_SCALE)
            total = jnp.sum(expo, axis=0, keepdims=True)
            mixed = lax.dot_general(expo.astype(jnp.bfloat16), vbufs[slot, at_keys, :], TN,
                                    preferred_element_type=jnp.float32)
            under = jnp.transpose(jnp.broadcast_to(total, (TOK, TOK)))
            outb[half, x, h] = (mixed / under).astype(jnp.bfloat16)

    def heads_of(xs, h):
        for slot, x in enumerate(xs):
            project(x, h, slot)
        for slot, x in enumerate(xs):
            attend(x, h, slot)

    def out_copies(x, h):
        mine = pl.multiple_of(((2 * x + core) * HEADS_EACH + h) * VDIM, VDIM)
        slot = x * HEADS_EACH + h
        spot = out_ref.at[:, pl.ds(mine, VDIM)]
        local = pltpu.make_async_copy(outb.at[core, x, h], spot, out_sem.at[slot])
        away = pltpu.make_async_remote_copy(
            src_ref=outb.at[other, x, h], dst_ref=spot,
            send_sem=give_sem.at[slot], recv_sem=take_sem.at[slot],
            device_id={"c": other}, device_id_type=pl.DeviceIdType.MESH,
        )
        return local, away

    def put_out(done):
        for x, h in done:
            for c in out_copies(x, h):
                c.start()

    pl.semaphore_wait(barrier, len(greeted))
    sent, finished, state = [], [], set()
    for what, name in order:
        if what == "load":
            for c in loads[:early]:
                c.wait()
        elif what == "send":
            for c in copies(name):
                c.start()
            sent.append(name)
        elif what == "wait":
            if "bias" not in state:
                make_bias()
                state.add("bias")
            for c in copies(name):
                c.wait_recv()
        elif what == "head":
            if "prepared" not in state:
                for c in loads[early:]:
                    c.wait()
                prepare()
                state.add("prepared")
            kind, h, steps = name
            if kind == "a":
                xs = [at("x", dx) for dx in steps]
                heads_of(xs, h)
            else:
                xs = list(range(NX))
                lax.fori_loop(0, NX // 2, lambda i, _: (heads_of([2 * i, 2 * i + 1], h), 0)[1], 0)
            put_out(finished)
            finished = [(x, h) for x in xs]
    put_out(finished)
    for name in sent:
        for c in copies(name):
            c.wait_send()
    for x in range(NX):
        for h in range(HEADS_EACH):
            local, away = out_copies(x, h)
            local.wait()
            away.wait()


def shards(queries, latent, rope_keys, key_weight, value_weight, doc_lengths):
    weights, ready = weight_transfers()
    rest, lat_names = other_transfers()
    transfers = rest[:2] + weights + rest[2:]
    after = lat_names + [t.name for t in rest if t.kind == "q"] + ["load"]
    units = [(k, v + after, UNIT_US[NX if k[2] is None else len(k[2])]) for k, v in ready.items()]
    order = plan(transfers, units, depth=DEPTH)[0]
    index, at = {}, 0
    for t in transfers:
        index[t.name] = at
        at += 2 if t.kind == "lat" else 1
    parts = {t.name: t for t in transfers}
    hbm = pl.BlockSpec(memory_space=pl.ANY)
    bf = jnp.bfloat16
    return pl.pallas_call(
        functools.partial(kernel, order, index, parts),
        out_shape=jax.ShapeDtypeStruct((TOK, 64 * VDIM), bf),
        in_specs=[hbm] * 5 + [pl.BlockSpec(memory_space=pltpu.VMEM)],
        out_specs=hbm,
        scratch_shapes=[
            pltpu.VMEM((NX, HEADS_EACH, NZ, NY, SLAB, 2 * NOPE), bf),
            pltpu.VMEM((NX, NC, TOK, 4 * PAIR), bf),
            pltpu.VMEM((6, TOK, LATENT), bf),
            pltpu.VMEM((6, ROPE, TOK), bf),
            pltpu.VMEM((KEYS, 128), bf),
            pltpu.VMEM((4, KEYS, 256), bf),
            pltpu.VMEM((2, KEYS, VDIM), bf),
            pltpu.VMEM((NC, WIN, TOK), jnp.float32),
            pltpu.VMEM((NC, NX, HEADS_EACH, TOK, VDIM), bf),
            pltpu.SemaphoreType.DMA((at,)),
            pltpu.SemaphoreType.DMA((at,)),
            pltpu.SemaphoreType.DMA((2 * HEADS_EACH + 2 + NX,)),
            pltpu.SemaphoreType.DMA((NX * HEADS_EACH,)),
            pltpu.SemaphoreType.DMA((NX * HEADS_EACH,)),
            pltpu.SemaphoreType.DMA((NX * HEADS_EACH,)),
        ],
        compiler_params=pltpu.CompilerParams(
            collective_id=0, has_side_effects=True, vmem_limit_bytes=56 * 2**20
        ),
    )(queries, latent, rope_keys.T, key_weight, value_weight, doc_lengths.reshape(1, -1))


def solution(mesh):
    torus = Mesh(mesh.devices.reshape(NZ, NY, NX, NC), ("z", "y", "x", "c"))
    rows = P(("z", "y", "x", "c"), None)
    weight = P(("z", "y"), ("x", "c"))
    return jax.shard_map(
        shards, mesh=torus, in_specs=(rows, rows, rows, weight, weight, P()), out_specs=rows,
        check_vma=False,
    )
```

time: 103 us -> 75.6 us (0.73)
  Pallas kernels: 98.2 us -> 72.4 us
  local copies, waits for them, and re-layouts: 4.53 us -> 3.1 us
    pallas_call x1, Pallas kernels: 98.2 us -> 72.4 us  [shards(): pl.pallas_call(functools.partial(kernel, order, index, parts), out_shape=...]
    unnamed x2 -> x1, local copies, waits for them, and re-layouts: 4.53 us -> 3.1 us
where the time goes in v2:
time: 75.6 us; the launch traced here: 75.5 us
  Pallas kernels  72.4 us (96%)
  local copies, waits for them, and re-layouts  3.1 us (4%)
    pallas_call x1, Pallas kernels, shards(): pl.pallas_call(functools.partial(kernel, order, index, parts), out_shape=...  72.4 us
    unnamed x1, local copies, waits for them, and re-layouts  3.1 us

profile of v2, /device:TPU:1, one launch (start us, length us, event | category | flops | bytes accessed | tf_op | source)
XLA Modules:
  0.0 75.5 jit_solution(2546202311853928889)
XLA Ops:
  0.0 72.4 %shard_map.64 = bf16[128,8192]{1,0:T(8,128)(2,1)} custom-call(bf16[128,12288]{1,0:T(8,128)(2,1)} %q_ref.1, bf16[128,512]{1,0:T(8,128)(2,1)} %lat_ref.1, bf16[64,128]{1,0:T(8,128)(2,1)} %bitcast.2, bf16[16,1024]{1,0:T(8,128)(2,1)} %kw_ref.1, bf16[16,1024]{1,0:T(8,128)(2,1)} %vw_ref.1, s32[1,128]{1,0:T(1,128)} %bitcast.3), custom_call_target="tpu_custom_call" | custom-call | tf_op jit(solution)/shard_map/pallas_call | solution.py:428
  72.4 3.1 %copy.8 = bf16[128,8192]{1,0:T(8,128)(2,1)} copy(bf16[128,8192]{1,0:T(8,128)(2,1)} %shard_map.64) | data formatting | bytes 4194304

commit v3 on v2

--- a/solution.py
+++ b/solution.py
@@ -25,26 +25,52 @@
 SIZES = {"x": NX, "y": NY, "z": NZ}
 FULL = {"x": (0, NX), "y": (0, NY), "z": (0, NZ)}
 
-X_LAST = (0, 1, 2)
-Y_LAST = (5, 4, 3)
-Z_LAST = (6, 7)
-LATER = (1, 4)
-FINE = (True, False, False)
-X_FORWARD = 3
-DEPTH = 4.0
-UNIT_US = {1: 1.1, 2: 1.5, 4: 3.0}
+FIRST = [
+    ('b', (4, 1), 'x', 'direct', 1),
+    ('a', (0, 1), 'z', 'direct', 1),
+    ('B', (5, 1), 'z', 'direct', -1),
+    ('c', (6, 2), 'x', 'direct', -1),
+    ('l', (1, 3), 'z', 'ring', 1),
+]
+CHAINS = [
+    ('a0', 'a', (0, 1), 'zyx', True, ('z', 'z'), 3),
+    ('b0', 'B', (5, 1), 'zxy', True, ('z', 'z'), None),
+    ('c', 'c', (6, 1), 'xyz', False, ('x', 'x'), None),
+    ('d', 'c', (7, 1), 'xyz', False, ('x', 'x'), None),
+    ('a1', 'l', (1, 1), 'zyx', False, ('z', 'z'), 3),
+    ('b1', 'b', (4, 1), 'xzy', False, ('x', 'x'), None),
+    ('a2', 'l', (2, 1), 'zyx', True, ('z', 'z'), 3),
+    ('b2', 'l', (3, 1), 'zxy', False, ('z', 'z'), None),
+]
+DEPTH = 4
+LATE = 0.0
+FIXED_US = 1.4
+HOP_US = 0.9
+UNIT_US = {1: 1.15, 2: 1.55, 4: 2.6}
 NT = (((1,), (1,)), ((), ()))
 TN = (((0,), (0,)), ((), ()))
 
 
+ORDER = {"fb": -19.4, "fa": -6.0, "fB": -14.9, "fc": -20.8, "fl": -6.7, "a0": -4.4, "a0h0": -0.6, "b0": -5.2, "b0h5": 17.1, "c": 2.0, "ch6": 0.9, "d": 2.7, "dh7": 15.9, "a1": -11.2, "a1h1": 24.8, "b1": -1.6, "b1h4": 10.0, "a2": -19.8, "a2h2": 3.3, "b2": -14.1, "b2h3": 22.7, "lat": -19.1, "q": 9.6}
+REACH_SHARE = 0.6
+
+
+def stage(name):
+    if name[0] == "f":
+        return name[:2]
+    if name[0] in "lq":
+        return "lat" if name[0] == "l" else "q"
+    return name[:name.index("u")] if "u" in name else name[:-3]
+
+
 def PRIORITY(t, reach):
-    return 0
+    return ORDER[stage(t.name)] - REACH_SHARE * reach
 
 
 class Transfer:
-    def __init__(self, name, kind, where, target, deps, link, size, hops=1):
+    def __init__(self, name, kind, where, target, deps, link, size, hops=1, late=0.0):
         self.name, self.kind, self.where, self.target = name, kind, where, target
-        self.deps, self.link, self.size, self.hops = list(deps), link, size, hops
+        self.deps, self.link, self.size, self.hops, self.late = list(deps), link, size, hops, late
 
 
 def weight_transfers():
@@ -73,7 +99,7 @@
     def ring(tag, axis, spot, heads, deps, half_axis, forward=None):
         n = SIZES[axis]
         got = {0: list(deps)}
-        lo, width = heads if half_axis == "h" else spot[half_axis]
+        lo, width = heads if half_axis == "h" else spot.get(half_axis, (0, 2))
         cut = width // 2 if forward is None else forward
         for sign in (1, -1):
             last = list(deps)
@@ -86,58 +112,49 @@
                         continue
                     if half_axis == "h":
                         part = share
-                    else:
+                    elif half_axis:
                         piece[half_axis] = share
                 name = add(f"{tag}{axis}{'+' if sign > 0 else '-'}{k}", piece, part, (axis, sign), last)
                 last = [name]
                 got.setdefault(n // 2 if k == n // 2 else -sign * k, []).append(name)
         return got
 
-    def last_ring(tag, axis, inner, spot, heads, units, forward=None):
+    def last_ring(tag, axis, inner, spot, heads, units, half_axis, forward=None):
         got = {}
         for offset, deps in units.items():
-            piece = dict(spot)
+            piece, way = dict(spot), forward
             if offset is None:
                 piece[inner] = FULL[inner]
             else:
                 piece[inner] = ("at", offset)
-            for o, names in ring(f"{tag}u{offset}", axis, piece, heads, deps, "z", forward).items():
+            for o, names in ring(f"{tag}u{offset}", axis, piece, heads, deps, half_axis, way).items():
                 got.setdefault(o, []).extend(names)
         return {o: sorted(set(names)) for o, names in got.items()}
 
-    def whole(units):
+    def merged(units):
         return {None: sorted(set(sum(units.values(), [])))}
 
     local = ["load"]
-    first = {X_LAST[0]: direct("f0", "z", (X_LAST[0], 1), local, 1),
-             Y_LAST[0]: direct("f1", "z", (Y_LAST[0], 1), local, -1)}
-    zl = (Z_LAST[0], len(Z_LAST))
-    c_first = direct("fc", "x", zl, local, -1)
-    later = ring("f2", "z", own(), LATER, local, "h")
-    later = sorted(set(sum(later.values(), [])))
-    for h in X_LAST[1:] + Y_LAST[1:]:
-        first[h] = later
-    c_units = ring("c", "y", own(x=FULL["x"]), zl, c_first + local, "x")
-    c_all = whole(c_units)[None]
-    for i in range(3):
-        h = X_LAST[i]
-        units = ring(f"a{i}", "y", own(z=FULL["z"]), (h, 1), first[h] + local, "z")
-        if not FINE[i]:
-            units = whole(units)
-        got = last_ring(f"a{i}", "x", "y", own(z=FULL["z"]), (h, 1), units, X_FORWARD)
-        ready[("a", h, (0,))] = got[0]
-        ready[("a", h, (-1, 1))] = sorted(set(got[-1] + got[1]))
-        ready[("a", h, (2,))] = got[2]
-        h = Y_LAST[i]
-        units = ring(f"b{i}", "x", own(z=FULL["z"]), (h, 1), first[h] + local, "z")
-        if not FINE[i]:
-            units = whole(units)
-        got = last_ring(f"b{i}", "y", "x", own(z=FULL["z"]), (h, 1), units)
-        ready[("b", h, None)] = sorted(set(sum(got.values(), [])))
-        if i < 2:
-            h = Z_LAST[i]
-            got = ring(f"c{i}", "z", own(x=FULL["x"], y=FULL["y"]), (h, 1), c_all, "x")
-            ready[("c", h, None)] = sorted(set(sum(got.values(), [])))
+    first = {}
+    for tag, heads, axis, how, far in FIRST:
+        if how == "direct":
+            names = direct(f"f{tag}", axis, heads, local, far)
+        else:
+            names = sorted(set(sum(ring(f"f{tag}", axis, own(), heads, local, "h").values(), [])))
+        first[tag] = names + local
+    for tag, source, heads, axes, fine, halves, forward in CHAINS:
+        a, b, c = axes
+        units = ring(f"{tag}", b, own(**{a: FULL[a]}), heads, first[source], halves[0])
+        if not fine:
+            units = merged(units)
+        for h in range(heads[0], heads[0] + heads[1]):
+            got = last_ring(f"{tag}h{h}", c, b, own(**{a: FULL[a]}), (h, 1), units, halves[1], forward)
+            if c == "x":
+                ready[("a", h, (0,))] = got[0]
+                ready[("a", h, (-1, 1))] = sorted(set(got[-1] + got[1]))
+                ready[("a", h, (2,))] = got[2]
+            else:
+                ready[("b", h, None)] = sorted(set(sum(got.values(), [])))
     return out, ready
 
 
@@ -145,9 +162,9 @@
     lat = TOK * (LATENT + 64) * 2
     q = TOK * 4 * PAIR * 2
     out = [
-        Transfer("lat.next", "lat", ("in", 2), "next", [], "x+", lat),
+        Transfer("lat.next", "lat", ("in", 2), "next", [], "x+", lat, 1, LATE),
         Transfer("lat.core", "lat", ("in", 4), "core", [], "c", lat),
-        Transfer("lat.next2", "lat", (2, 0), "next", ["lat.next"], "x+", lat),
+        Transfer("lat.next2", "lat", (2, 0), "next", ["lat.next"], "x+", lat, 1, LATE),
         Transfer("lat.core1", "lat", (2, 2), "core", ["lat.next"], "c", lat),
         Transfer("lat.core2", "lat", (0, 0), "core", ["lat.next2"], "c", lat),
     ]
@@ -157,10 +174,9 @@
     return out, lat_names
 
 
-def plan(transfers, units, rate=46.6e3, d2d=600e3, depth=4.0):
+def plan(transfers, units, rate=45e3, d2d=500e3, depth=4.0):
     by_name = {t.name: t for t in transfers}
-    tail = {}
-    follow = {}
+    tail, follow = {}, {}
     for t in transfers:
         for d in t.deps:
             follow.setdefault(d, []).append(t.name)
@@ -168,9 +184,12 @@
     def cost(t):
         return t.size * t.hops / (d2d if t.link == "c" else rate)
 
+    def delay(t):
+        return FIXED_US + HOP_US * t.hops + t.late
+
     def reach(name):
         if name not in tail:
-            tail[name] = cost(by_name[name]) + 1.0 + 0.75 * by_name[name].hops + max(
+            tail[name] = cost(by_name[name]) + delay(by_name[name]) + max(
                 [reach(f) for f in follow.get(name, [])], default=0.0)
         return tail[name]
 
@@ -185,7 +204,7 @@
                 if free.get(t.link, 0.0) - now > depth:
                     continue
                 free[t.link] = max(now, free.get(t.link, 0.0)) + cost(t)
-                arrive[t.name] = free[t.link] + 1.0 + 0.75 * t.hops
+                arrive[t.name] = free[t.link] + delay(t)
                 sent.add(t.name)
                 order.append(("send", t.name))
 
@@ -193,12 +212,15 @@
     seen.add("load")
     issue()
     todo = list(units)
-    busy = 0.0
     while todo or len(seen) <= len(transfers):
         waiting = sorted((when, name) for name, when in arrive.items() if name not in seen)
         unit = next((u for u in todo if all(d in seen for d in u[1])), None)
         if waiting and (waiting[0][0] <= now or unit is None):
             when, name = waiting[0]
+            if when > now + 0.5 and any(t.name not in sent and all(d in seen for d in t.deps) for t in transfers):
+                now += 0.5
+                issue()
+                continue
             now = max(now, when)
             seen.add(name)
             order.append(("wait", name))
@@ -207,16 +229,15 @@
             todo.remove(unit)
             order.append(("head", unit[0]))
             now += unit[2]
-            busy += unit[2]
             issue()
         else:
             now += 0.2
             issue()
-    return order, now, max(arrive.values(), default=0), busy
+    return order, now, max(arrive.values(), default=0.0)
 
 
 def kernel(order, index, parts, q_ref, lat_ref, rope_ref, kw_ref, vw_ref, len_ref, out_ref,
-           wbuf, qb, latb, ropeb, rope2, kexts, vbufs, bias, outb,
+           wbuf, qb, latb, ropeb, kexts, vbufs, bias, outb,
            send_sem, recv_sem, load_sem, out_sem, give_sem, take_sem):
     me = {a: lax.axis_index(a) for a in "xyz"}
     core = lax.axis_index("c")
@@ -293,7 +314,7 @@
             for i, (s, d) in enumerate(pairs)
         ]
 
-    lane = lax.broadcasted_iota(jnp.int32, (KEYS, 128), 1)
+    lane = lax.broadcasted_iota(jnp.int32, (TOK, 128), 1)
 
     def make_bias():
         lens = len_ref[...].astype(jnp.float32)
@@ -315,21 +336,32 @@
             r = ropeb[s].astype(jnp.float32)
             r = jnp.transpose(jnp.concatenate([r, r], axis=0))
             spot = pl.ds(s * TOK, TOK)
-            rope2[spot, :] = r.astype(jnp.bfloat16)
-            for slot in range(2):
-                kexts[2 * slot, spot, NOPE:] = jnp.where(lane[:TOK] < ROPE, r, 0.0).astype(jnp.bfloat16)
+            low = lane < ROPE
+            for slot in range(4):
+                kexts[2 * slot, spot, NOPE:] = jnp.where(low, r, 0.0).astype(jnp.bfloat16)
+                kexts[2 * slot + 1, spot, :NOPE] = jnp.where(low, 0.0, r).astype(jnp.bfloat16)
+        for slot in range(4):
+            vbufs[slot, :, VDIM:] = jnp.ones((KEYS, VDIM), jnp.bfloat16)
+
+        def order_queries(i, carry):
+            x, half = i // NC, lax.rem(i, NC)
+            for pair in range(HEADS_EACH // 2):
+                mid = qb[x, half, :, pl.ds(pair * PAIR + 128, 128)].astype(jnp.float32)
+                end = qb[x, half, :, pl.ds(pair * PAIR + 256, 128)].astype(jnp.float32)
+                low = lane < ROPE
+                qb[x, half, :, pl.ds(pair * PAIR + 128, 128)] = jnp.where(low, mid, end).astype(jnp.bfloat16)
+                turned = pltpu.roll(jnp.where(low, end, mid), ROPE, 1)
+                qb[x, half, :, pl.ds(pair * PAIR + 256, 128)] = turned.astype(jnp.bfloat16)
+            return carry
+
+        lax.fori_loop(0, NX * NC, order_queries, 0)
 
     def project(x, h, slot):
         w = wbuf[x, h].reshape(LATENT, 2 * NOPE)
         kv = jnp.dot(latb[...].reshape(KEYS, LATENT), w, preferred_element_type=jnp.float32)
-        keys = kv[:, :NOPE]
-        vbufs[slot] = kv[:, NOPE:].astype(jnp.bfloat16)
-        if h % 2 == 0:
-            kexts[2 * slot, :, :NOPE] = keys.astype(jnp.bfloat16)
-        else:
-            turned = pltpu.roll(keys, 64, 1)
-            kexts[2 * slot + 1, :, :NOPE] = jnp.where(lane < 64, 0.0, turned).astype(jnp.bfloat16)
-            kexts[2 * slot + 1, :, NOPE:] = jnp.where(lane < 64, turned.astype(jnp.bfloat16), rope2[...])
+        vbufs[slot, :, :VDIM] = kv[:, NOPE:].astype(jnp.bfloat16)
+        place = slice(NOPE, 2 * NOPE) if h % 2 else slice(0, NOPE)
+        kexts[2 * slot + h % 2, :, place] = kv[:, :NOPE].astype(jnp.bfloat16)
 
     def attend(x, h, slot):
         column = (h // 2) * PAIR + (h % 2) * 128
@@ -340,11 +372,9 @@
             s = scores[at_keys, at_rows] + bias[half]
             peak = jnp.max(s, axis=0, keepdims=True)
             expo = jnp.exp2((s - peak) * EXP_SCALE)
-            total = jnp.sum(expo, axis=0, keepdims=True)
             mixed = lax.dot_general(expo.astype(jnp.bfloat16), vbufs[slot, at_keys, :], TN,
                                     preferred_element_type=jnp.float32)
-            under = jnp.transpose(jnp.broadcast_to(total, (TOK, TOK)))
-            outb[half, x, h] = (mixed / under).astype(jnp.bfloat16)
+            outb[half, x, h] = (mixed[:, :VDIM] / mixed[:, VDIM:]).astype(jnp.bfloat16)
 
     def heads_of(xs, h):
         for slot, x in enumerate(xs):
@@ -397,7 +427,7 @@
                 heads_of(xs, h)
             else:
                 xs = list(range(NX))
-                lax.fori_loop(0, NX // 2, lambda i, _: (heads_of([2 * i, 2 * i + 1], h), 0)[1], 0)
+                heads_of(xs, h)
             put_out(finished)
             finished = [(x, h) for x in xs]
     put_out(finished)
@@ -414,7 +444,7 @@
 def shards(queries, latent, rope_keys, key_weight, value_weight, doc_lengths):
     weights, ready = weight_transfers()
     rest, lat_names = other_transfers()
-    transfers = rest[:2] + weights + rest[2:]
+    transfers = weights + rest
     after = lat_names + [t.name for t in rest if t.kind == "q"] + ["load"]
     units = [(k, v + after, UNIT_US[NX if k[2] is None else len(k[2])]) for k, v in ready.items()]
     order = plan(transfers, units, depth=DEPTH)[0]
@@ -435,9 +465,8 @@
             pltpu.VMEM((NX, NC, TOK, 4 * PAIR), bf),
             pltpu.VMEM((6, TOK, LATENT), bf),
             pltpu.VMEM((6, ROPE, TOK), bf),
-            pltpu.VMEM((KEYS, 128), bf),
-            pltpu.VMEM((4, KEYS, 256), bf),
-            pltpu.VMEM((2, KEYS, VDIM), bf),
+            pltpu.VMEM((8, KEYS, 256), bf),
+            pltpu.VMEM((4, KEYS, 2 * VDIM), bf),
             pltpu.VMEM((NC, WIN, TOK), jnp.float32),
             pltpu.VMEM((NC, NX, HEADS_EACH, TOK, VDIM), bf),
             pltpu.SemaphoreType.DMA((at,)),

time: 75.6 us -> 69.9 us (0.925)
  Pallas kernels: 72.4 us -> 66.7 us
    pallas_call x1, Pallas kernels: 72.4 us -> 66.7 us  [shards(): pl.pallas_call(functools.partial(kernel, order, index, parts), out_shape=...]
where the time goes in v3:
time: 69.9 us; the launch traced here: 69.8 us
  Pallas kernels  66.7 us (95%)
  local copies, waits for them, and re-layouts  3.1 us (4%)
    pallas_call x1, Pallas kernels, shards(): pl.pallas_call(functools.partial(kernel, order, index, parts), out_shape=...  66.7 us
    unnamed x1, local copies, waits for them, and re-layouts  3.1 us

profile of v3, /device:TPU:1, one launch (start us, length us, event | category | flops | bytes accessed | tf_op | source)
XLA Modules:
  0.0 69.8 jit_solution(8104499434163701933)
XLA Ops:
  0.0 66.7 %shard_map.64 = bf16[128,8192]{1,0:T(8,128)(2,1)} custom-call(bf16[128,12288]{1,0:T(8,128)(2,1)} %q_ref.1, bf16[128,512]{1,0:T(8,128)(2,1)} %lat_ref.1, bf16[64,128]{1,0:T(8,128)(2,1)} %bitcast.2, bf16[16,1024]{1,0:T(8,128)(2,1)} %kw_ref.1, bf16[16,1024]{1,0:T(8,128)(2,1)} %vw_ref.1, s32[1,128]{1,0:T(1,128)} %bitcast.3), custom_call_target="tpu_custom_call" | custom-call | tf_op jit(solution)/shard_map/pallas_call | solution.py:458
  66.7 3.1 %copy.8 = bf16[128,8192]{1,0:T(8,128)(2,1)} copy(bf16[128,8192]{1,0:T(8,128)(2,1)} %shard_map.64) | data formatting | bytes 4194304

commit v4 on v3

--- a/solution.py
+++ b/solution.py
@@ -42,7 +42,7 @@
     ('a2', 'l', (2, 1), 'zyx', True, ('z', 'z'), 3),
     ('b2', 'l', (3, 1), 'zxy', False, ('z', 'z'), None),
 ]
-DEPTH = 4
+DEPTH = 8.0
 LATE = 0.0
 FIXED_US = 1.4
 HOP_US = 0.9
@@ -331,30 +331,36 @@
             q_row = (base + lax.broadcasted_iota(jnp.int32, (WIN, TOK), 1)).astype(jnp.float32)
             bias[half] = jnp.where((k_pos >= q_start) & (k_pos <= q_row), 0.0, LOWEST)
 
-    def prepare():
-        for s in range(6):
-            r = ropeb[s].astype(jnp.float32)
-            r = jnp.transpose(jnp.concatenate([r, r], axis=0))
-            spot = pl.ds(s * TOK, TOK)
-            low = lane < ROPE
-            for slot in range(4):
-                kexts[2 * slot, spot, NOPE:] = jnp.where(low, r, 0.0).astype(jnp.bfloat16)
-                kexts[2 * slot + 1, spot, :NOPE] = jnp.where(low, 0.0, r).astype(jnp.bfloat16)
+    low = lane < ROPE
+
+    def make_ones():
         for slot in range(4):
             vbufs[slot, :, VDIM:] = jnp.ones((KEYS, VDIM), jnp.bfloat16)
 
-        def order_queries(i, carry):
-            x, half = i // NC, lax.rem(i, NC)
-            for pair in range(HEADS_EACH // 2):
-                mid = qb[x, half, :, pl.ds(pair * PAIR + 128, 128)].astype(jnp.float32)
-                end = qb[x, half, :, pl.ds(pair * PAIR + 256, 128)].astype(jnp.float32)
-                low = lane < ROPE
-                qb[x, half, :, pl.ds(pair * PAIR + 128, 128)] = jnp.where(low, mid, end).astype(jnp.bfloat16)
-                turned = pltpu.roll(jnp.where(low, end, mid), ROPE, 1)
-                qb[x, half, :, pl.ds(pair * PAIR + 256, 128)] = turned.astype(jnp.bfloat16)
-            return carry
-
-        lax.fori_loop(0, NX * NC, order_queries, 0)
+    def place_rope(s):
+        r = ropeb[s].astype(jnp.float32)
+        r = jnp.transpose(jnp.concatenate([r, r], axis=0))
+        spot = pl.ds(pl.multiple_of(s * TOK, TOK), TOK)
+        first = jnp.where(low, r, 0.0).astype(jnp.bfloat16)
+        second = jnp.where(low, 0.0, r).astype(jnp.bfloat16)
+        for slot in range(4):
+            kexts[2 * slot, spot, NOPE:] = first
+            kexts[2 * slot + 1, spot, :NOPE] = second
+
+    def order_queries(x, half):
+        for pair in range(HEADS_EACH // 2):
+            mid = qb[x, half, :, pl.ds(pair * PAIR + 128, 128)].astype(jnp.float32)
+            end = qb[x, half, :, pl.ds(pair * PAIR + 256, 128)].astype(jnp.float32)
+            qb[x, half, :, pl.ds(pair * PAIR + 128, 128)] = jnp.where(low, mid, end).astype(jnp.bfloat16)
+            turned = pltpu.roll(jnp.where(low, end, mid), ROPE, 1)
+            qb[x, half, :, pl.ds(pair * PAIR + 256, 128)] = turned.astype(jnp.bfloat16)
+
+    def settle(name):
+        if name[0] == "q":
+            order_queries(parts[name].where, other)
+        elif name[0] == "l":
+            place_rope({"lat.core": 4 + other, "lat.next": 2 + core, "lat.core1": 2 + other,
+                        "lat.next2": core, "lat.core2": other}[name])
 
     def project(x, h, slot):
         w = wbuf[x, h].reshape(LATENT, 2 * NOPE)
@@ -400,8 +406,11 @@
                 c.start()
 
     pl.semaphore_wait(barrier, len(greeted))
-    sent, finished, state = [], [], set()
+    sent, finished, arrived, state = [], [], [], set()
     for what, name in order:
+        if what != "send":
+            while arrived:
+                settle(arrived.pop())
         if what == "load":
             for c in loads[:early]:
                 c.wait()
@@ -410,17 +419,19 @@
                 c.start()
             sent.append(name)
         elif what == "wait":
-            if "bias" not in state:
+            if "own" not in state:
                 make_bias()
-                state.add("bias")
+                make_ones()
+                for c in loads[early:]:
+                    c.wait()
+                place_rope(4 + core)
+                for x in range(NX):
+                    order_queries(x, core)
+                state.add("own")
             for c in copies(name):
                 c.wait_recv()
+            arrived.append(name)
         elif what == "head":
-            if "prepared" not in state:
-                for c in loads[early:]:
-                    c.wait()
-                prepare()
-                state.add("prepared")
             kind, h, steps = name
             if kind == "a":
                 xs = [at("x", dx) for dx in steps]

time: 69.9 us -> 69.8 us (level)
  no operation moved by 1% of the time
where the time goes in v4:
time: 69.8 us; the launch traced here: 69.7 us
  Pallas kernels  66.6 us (95%)
  local copies, waits for them, and re-layouts  3.1 us (4%)
    pallas_call x1, Pallas kernels, shards(): pl.pallas_call(functools.partial(kernel, order, index, parts), out_shape=...  66.6 us
    unnamed x1, local copies, waits for them, and re-layouts  3.1 us

profile of v4, /device:TPU:1, one launch (start us, length us, event | category | flops | bytes accessed | tf_op | source)
XLA Modules:
  0.0 69.7 jit_solution(6193485729368039997)
XLA Ops:
  0.0 66.6 %shard_map.64 = bf16[128,8192]{1,0:T(8,128)(2,1)} custom-call(bf16[128,12288]{1,0:T(8,128)(2,1)} %q_ref.1, bf16[128,512]{1,0:T(8,128)(2,1)} %lat_ref.1, bf16[64,128]{1,0:T(8,128)(2,1)} %bitcast.2, bf16[16,1024]{1,0:T(8,128)(2,1)} %kw_ref.1, bf16[16,1024]{1,0:T(8,128)(2,1)} %vw_ref.1, s32[1,128]{1,0:T(1,128)} %bitcast.3), custom_call_target="tpu_custom_call" | custom-call | tf_op jit(solution)/shard_map/pallas_call | solution.py:469
  66.6 3.1 %copy.8 = bf16[128,8192]{1,0:T(8,128)(2,1)} copy(bf16[128,8192]{1,0:T(8,128)(2,1)} %shard_map.64) | data formatting | bytes 4194304
